TPU v7x, 512 devices: a whole 4x4x16 slice. The times are simulated.
512 devices in a mesh: depth: 16 (over z), tx: 8 (over x, core), ty: 4 (over y).
Axes of the slice: x: 4, y: 4, z: 16, core: 2. Of those that a mesh axis runs over, the one named last changes fastest.
Arguments:
- slices: float32 [16, 2, 2048, 1024], P('depth', None, 'tx', 'ty'), may hold values from -1.15 to 1.15
- thickness: float32 [16], P('depth'), may hold values from 0.1 to 0.6
- probes: float32 [8, 2, 128, 128], replicated, may hold values from -4 to 4
- centers: int32 [8, 4, 12, 2], P('tx', 'ty'), may hold values from 0 to 255
- batch_of: int32 [8, 4, 12, 1], P('tx', 'ty'), may hold values from 0 to 7; in each aligned block of 12 rows (0 to 11, 12 to 23, ..., all dimensions but the last counted through in order) at most 2 rows name the same one
- intensity: float32 [8, 4, 12, 128, 128], P('tx', 'ty'), may hold values from 0 to 2
Outputs:
- gradient: float32 [16, 2, 2048, 1024], P('depth', None, 'tx', 'ty')
Inputs may be any that keep to these rules, and one draw needn't show every extreme that they name: `batch_of`: among the windows of one tile, no micro-batch appears more than 2 times.
All inputs are finite; a program needn't handle non-finite values.
Results may differ from a plain program's by a relative error of at most 0.0003.
Values sent between devices are 32-bit elements; how exact they have to be, the bound alone decides.
A program may use at most 64 MiB of HBM per device.

v0:
```python
import math

import jax
import jax.numpy as jnp
from jax import lax
from jax.sharding import PartitionSpec as P

HIGHEST = lax.Precision.HIGHEST


def padded_2(block, sides, width):
    for axis, dim in sides:
        count = lax.axis_size(axis)
        forward = [(i, i + 1) for i in range(count - 1)]
        forward.append((count - 1, 0))
        backward = [(target, source) for source, target in forward]
        low = lax.ppermute(
            lax.slice_in_dim(block, block.shape[dim] - width, None, axis=dim), axis, forward
        )
        high = lax.ppermute(lax.slice_in_dim(block, 0, width, axis=dim), axis, backward)
        block = jnp.concatenate([low, block, high], axis=dim)
    return block


def dft_tables(length):
    counts = jnp.arange(length, dtype=jnp.int32)
    product = counts[:, None] * counts[None, :] % length
    angles = product.astype(jnp.float32) * (2.0 * math.pi / length)
    factor = 1.0 / math.sqrt(length)
    return (jnp.cos(angles) * factor, jnp.sin(angles) * factor)


def transform(planes, cosine_table, sine_table, direction):
    imag_table = -direction * sine_table
    left_real = jnp.einsum("jk,pskl->psjl", cosine_table, planes, precision=HIGHEST)
    left_imag = jnp.einsum("jk,pskl->psjl", imag_table, planes, precision=HIGHEST)
    halfway = jnp.stack([left_real[0] - left_imag[1], left_real[1] + left_imag[0]])
    right_real = jnp.einsum("psjk,kl->psjl", halfway, cosine_table, precision=HIGHEST)
    right_imag = jnp.einsum("psjk,kl->psjl", halfway, imag_table, precision=HIGHEST)
    return jnp.stack([right_real[0] - right_imag[1], right_real[1] + right_imag[0]])


def multiply(first, second):
    return jnp.stack(
        [first[0] * second[0] - first[1] * second[1], first[0] * second[1] + first[1] * second[0]]
    )


def conj_multiply(first, second):
    return jnp.stack(
        [first[0] * second[0] + first[1] * second[1], first[0] * second[1] - first[1] * second[0]]
    )


def local(slices, thickness, probes, centers, batch_of, intensity):
    sections = lax.axis_size("depth")
    my_section = lax.axis_index("depth")
    window = probes.shape[-1]
    half_width = window // 2
    cosine_table, sine_table = dft_tables(window)
    counts = jnp.arange(window, dtype=jnp.int32)
    offset = (counts + half_width) % window - half_width
    squares = offset[:, None] * offset[:, None] + offset[None, :] * offset[None, :]
    base_phase = squares.astype(jnp.float32) * (math.pi / (half_width * half_width))
    padded = padded_2(slices[0], (("tx", 1), ("ty", 2)), half_width)
    owners = batch_of[0, 0, :, 0]
    centre_table = centers[0, 0]
    windows_here = owners.shape[0]
    measured = intensity[0, 0]
    zero_index = jnp.int32(0)
    gradient_pad = jnp.zeros((2, padded.shape[1], padded.shape[2]), jnp.float32)
    per_device = -(-windows_here // sections)
    layout = jnp.arange(sections * per_device, dtype=jnp.int32).reshape(per_device, sections).T
    picked = jnp.minimum(layout, windows_here - 1)

    def cut_one(which):
        return lax.dynamic_slice(
            padded,
            (zero_index, centre_table[which, 0], centre_table[which, 1]),
            (2, window, window),
        )

    outgoing = jax.vmap(jax.vmap(cut_one))(picked)
    spread_thick = jnp.broadcast_to(thickness.reshape(1, 1), (sections, 1))
    arrived, all_thick = (
        lax.all_to_all(outgoing, "depth", split_axis=0, concat_axis=0, tiled=True),
        lax.all_to_all(spread_thick, "depth", split_axis=0, concat_axis=0, tiled=True),
    )
    layers = jnp.transpose(arrived, (0, 2, 1, 3, 4))
    mine = jnp.arange(per_device, dtype=jnp.int32) * sections + my_section
    mine_valid = (mine < windows_here).astype(jnp.float32)
    mine_clip = jnp.minimum(mine, windows_here - 1)
    start_wave = (
        jnp.transpose(probes[owners[mine_clip]], (1, 0, 2, 3)) * mine_valid[None, :, None, None]
    )

    def forward_layer(wave, inputs):
        patch_now, thick_now = inputs
        phase_now = thick_now * base_phase
        layer_kernel = jnp.stack([jnp.cos(phase_now), -jnp.sin(phase_now)])[:, None]
        spectrum = multiply(layer_kernel, transform(wave, cosine_table, sine_table, 1))
        incident = transform(spectrum, cosine_table, sine_table, -1)
        return (multiply(incident, patch_now), incident)

    leaving, incidents = lax.scan(forward_layer, start_wave, (layers, all_thick[:, 0]))
    detector = transform(leaving, cosine_table, sine_table, 1)
    target = measured[mine_clip]
    excess = 2.0 * (detector[0] * detector[0] + detector[1] * detector[1] - target)
    returning = transform(excess[None] * detector, cosine_table, sine_table, -1)

    def backward_layer(returning, inputs):
        patch_now, thick_now, incident = inputs
        phase_now = thick_now * base_phase
        layer_adjoint = jnp.stack([jnp.cos(phase_now), jnp.sin(phase_now)])[:, None]
        slice_term = conj_multiply(incident, returning)
        toward = conj_multiply(patch_now, returning)
        spectrum = multiply(layer_adjoint, transform(toward, cosine_table, sine_table, 1))
        return (transform(spectrum, cosine_table, sine_table, -1), slice_term)

    _, layer_terms = lax.scan(
        backward_layer, returning, (layers, all_thick[:, 0], incidents), reverse=True
    )
    sending = jnp.transpose(layer_terms, (0, 2, 1, 3, 4))
    received = lax.all_to_all(sending, "depth", split_axis=0, concat_axis=0, tiled=True)
    flat_terms = received.reshape(sections * per_device, 2, window, window)
    flat_index = picked.reshape(sections * per_device)
    flat_valid = (layout.reshape(sections * per_device) < windows_here).astype(jnp.float32)

    def place(which, gradient_pad):
        chosen_window = flat_index[which]
        corner = (zero_index, centre_table[chosen_window, 0], centre_table[chosen_window, 1])
        current = lax.dynamic_slice(gradient_pad, corner, (2, window, window))
        return lax.dynamic_update_slice(
            gradient_pad, current + flat_terms[which] * flat_valid[which], corner
        )

    gradient_pad = lax.fori_loop(0, sections * per_device, place, gradient_pad)
    row_rims = jnp.concatenate(
        [gradient_pad[:, :half_width], gradient_pad[:, -half_width:]], axis=1
    )
    beside_all = padded_2(row_rims, (("tx", 1),), half_width)
    inner = gradient_pad[:, half_width:-half_width]
    inner = inner.at[:, :half_width].add(beside_all[:, :half_width])
    inner = inner.at[:, -half_width:].add(beside_all[:, -half_width:])
    col_rims = jnp.concatenate([inner[:, :, :half_width], inner[:, :, -half_width:]], axis=2)
    beside = padded_2(col_rims, (("ty", 2),), half_width)
    result = inner[:, :, half_width:-half_width]
    result = result.at[:, :, :half_width].add(beside[:, :, :half_width])
    result = result.at[:, :, -half_width:].add(beside[:, :, -half_width:])
    return result[None]


def solution(mesh):
    placed = (
        P("depth", None, "tx", "ty"),
        P("depth"),
        P(),
        P("tx", "ty", None, None),
        P("tx", "ty", None, None),
        P("tx", "ty", None, None, None),
    )
    return jax.shard_map(
        local, mesh=mesh, in_specs=placed, out_specs=P("depth", None, "tx", "ty"), check_vma=False
    )
```

profile of v0, /device:TPU:1, one launch (start us, length us, event | category | flops | bytes accessed | tf_op | source)
XLA Modules:
  0.0 728.5 jit_solution(13357902879315080039)
XLA Ops:
  1.0 2.6 collective-permute-start
  3.6 4.3 collective-permute-start.1
  9.1 10.6 %all-to-all-start = ((f32[16,1,1]{2,1,0:T(1,128)}), f32[16,1,1]{2,1,0:T(1,128)S(1)}, u32[]{:S(2)}, u32[]{:S(2)}) async-start(f32[16,1,1]{2,1,0:T(1,128)} %broadcast_in_dim.53), calls=%async_computation | async-start | bytes 16384 | tf_op jit(solution)/shard_map/all_to_all | solution.py:87
  19.8 1.4 gather_fusion
  21.3 1.4 gather_fusion.1
  23.9 3.2 collective-permute-start.2
  27.1 3.4 collective-permute-start.3
  30.6 5.2 collective-permute-done.2
  35.7 1.6 collective-permute-done.3
  37.8 42.8 %while.54 = (s32[]{:T(128)}, f32[2,384,384]{2,1,0:T(8,128)S(1)}, s32[16,3]{0,1:T(4,128)S(1)}, f32[16,2,128,128]{2,3,1,0:T(8,128)}, s32[]{:T(128)}) while((s32[]{:T(128)}, f32[2,384,384]{2,1,0:T(8,128)S(1)}, s32[16,3]{0,1:T(4,128)S(1)}, f32[16,2,128,128]{2,3,1,0:T(8,128)}, s32[]{:T(128)}) %tuple.192), condition=%wide.while_cond.6, body=%wide.while_body.6.sunk | while | flops 2 | bytes 787057 | solution.py:77
  38.4 1.3 dynamic-slice_bitcast_fusion.4
  46.4 1.3 dynamic-slice_bitcast_fusion.4
  49.1 1.3 dynamic-slice_bitcast_fusion.4
  54.5 1.3 dynamic-slice_bitcast_fusion.4
  57.1 1.3 dynamic-slice_bitcast_fusion.4
  59.8 1.3 dynamic-slice_bitcast_fusion.4
  80.6 11.2 %all-to-all-start.1 = ((f32[16,1,2,128,128]{3,4,2,1,0:T(8,128)}), f32[16,1,2,128,128]{3,4,2,1,0:T(8,128)S(1)}, u32[]{:S(2)}, u32[]{:S(2)}) async-start(f32[16,1,2,128,128]{3,4,2,1,0:T(8,128)} %bitcast.454), calls=%async_computation.1 | async-start | bytes 4194304 | tf_op jit(solution)/shard_map/all_to_all | solution.py:86
  95.7 88.0 %all-to-all-done.1 = f32[16,1,2,128,128]{3,4,2,1,0:T(8,128)S(1)} async-done(((f32[16,1,2,128,128]{3,4,2,1,0:T(8,128)}), f32[16,1,2,128,128]{3,4,2,1,0:T(8,128)S(1)}, u32[]{:S(2)}, u32[]{:S(2)}) %all-to-all-start.1) | async-done | bytes 2097184 | tf_op jit(solution)/shard_map/all_to_all | solution.py:86
  183.7 111.6 %while.55 = (s32[]{:T(128)}, f32[2,1,128,128]{3,2,1,0:T(8,128)S(1)}, f32[16,2,1,128,128]{4,3,1,2,0:T(8,128)}, f32[16]{0:T(128)S(1)}, f32[16,2,1,128,128]{3,4,1,0...) while((s32[]{:T(128)}, ...), condition=%wide.region_1.2_spmd.clone.clone, body=%wide.region_0.1_spmd.clone.clone.sunk | while | flops 405274624 | bytes 4982457 | solution.py:105
  300.8 1.6 broadcast.294
  302.4 128.7 %while.56 = (s32[]{:T(128)}, f32[2,1,128,128]{3,2,1,0:T(8,128)S(1)}, f32[16,2,1,128,128]{3,4,1,2,0:T(8,128)}, f32[16]{0:T(128)S(1)}, f32[16,2,1,128,128]{3,4,2,1...) while((s32[]{:T(128)}, ...), condition=%wide.region_3.4_spmd.clone.clone, body=%wide.region_2.3_spmd.clone.clone.sunk | while | flops 405422080 | bytes 5637345 | solution.py:120
  431.1 11.2 %all-to-all-start.2 = ((f32[16,1,2,128,128]{3,4,2,1,0:T(8,128)}), f32[16,1,2,128,128]{3,4,2,1,0:T(8,128)S(1)}, u32[]{:S(2)}, u32[]{:S(2)}) async-start(f32[16,1,2,128,128]{3,4,2,1,0:T(8,128)} %bitcast.45), calls=%async_computation.2 | async-start | bytes 4194304 | tf_op jit(solution)/shard_map/all_to_all | solution.py:124
  442.3 91.9 %all-to-all-done.2 = f32[16,1,2,128,128]{3,4,2,1,0:T(8,128)S(1)} async-done(((f32[16,1,2,128,128]{3,4,2,1,0:T(8,128)}), f32[16,1,2,128,128]{3,4,2,1,0:T(8,128)S(1)}, u32[]{:S(2)}, u32[]{:S(2)}) %all-to-all-start.2) | async-done | bytes 2097184 | tf_op jit(solution)/shard_map/all_to_all | solution.py:124
  534.3 165.9 %while.53 = (s32[]{:T(128)}, f32[2,384,384]{2,1,0:T(8,128)S(1)}, s32[16]{0:T(128)S(1)}, s32[12,2]{0,1:T(2,128)S(1)}, f32[16,2,128,128]{2,3,1,0:T(8,128)S(1)}, /*...) while((s32[]{:T(128)}, f32[2,384,384]{2,1,0:T(8,128)S(1)}, s32[16]{0:T(128)S(1)}, ...), condition=%wide.region_5.6_spmd, body=%wide.region_4.5_spmd.sunk | while | flops 65547 | bytes 1179915 | solution.py:137
  542.3 2.5 dynamic_update_slice.29
  552.8 1.6 dynamic_update_slice.29
  562.4 2.5 dynamic_update_slice.29
  572.9 2.5 dynamic_update_slice.29
  583.4 2.4 dynamic_update_slice.29
  593.8 2.5 dynamic_update_slice.29
  604.3 2.5 dynamic_update_slice.29
  614.8 2.2 dynamic_update_slice.29
  625.0 2.3 dynamic_update_slice.29
  635.3 2.5 dynamic_update_slice.29
  645.9 2.1 dynamic_update_slice.29
  656.0 2.4 dynamic_update_slice.29
  666.5 2.4 dynamic_update_slice.29
  676.9 2.4 dynamic_update_slice.29
  687.3 2.4 dynamic_update_slice.29
  697.8 2.4 dynamic_update_slice.29
  700.3 5.5 collective-permute-start.4
  705.8 2.5 collective-permute-done.4
  708.4 2.5 collective-permute-done.5
  711.1 5.0 collective-permute-start.6
  716.3 3.5 collective-permute-start.7
  719.8 3.6 collective-permute-done.6
  724.7 1.6 collective-permute-done.7
  726.5 2.0 scatter-add.19
  (833 shorter events, 305.3 us)
Async XLA Ops:
  0.0 91.8 %copy-start = (s32[1,1,12,1]{2,3,1,0:T(1,128)S(1)}, s32[1,1,12,1]{2,3,1,0:T(1,128)}, u32[]{:S(2)}) copy-start(s32[1,1,12,1]{2,3,1,0:T(1,128)} %param.24) | copy-start | bytes 148
  1.0 21.6 %collective-permute-start = (f32[2,64,256]{2,1,0:T(8,128)S(1)}, f32[2,64,256]{2,1,0:T(8,128)S(1)}, u32[]{:S(2)}, u32[]{:S(2)}) collective-permute-start(f32[2,64,256]{2,1,0:T(8,128)S(1)} %get-tuple-element.722), channel_id=1, source_target_pairs={{0,4},{4,8},{8,12},{12,16},{16,20},{20,24},{24,28},{28,0},{1,5},{5... | collective-permute-start | bytes 393224 | tf_op jit(solution)/shard_map/ppermute | solution.py:17
  3.6 19.0 %collective-permute-start.1 = (f32[2,64,256]{2,1,0:T(8,128)S(1)}, f32[2,64,256]{2,1,0:T(8,128)S(1)}, u32[]{:S(2)}, u32[]{:S(2)}) collective-permute-start(f32[2,64,256]{2,1,0:T(8,128)S(1)} %get-tuple-element.723), channel_id=1, source_target_pairs={{4,0},{8,4},{12,8},{16,12},{20,16},{24,20},{28,24},{0,28},{5,1},{9... | collective-permute-start | bytes 393224 | tf_op jit(solution)/shard_map/ppermute | solution.py:20
  9.1 71.5 %all-to-all-start = ((f32[16,1,1]{2,1,0:T(1,128)}), f32[16,1,1]{2,1,0:T(1,128)S(1)}, u32[]{:S(2)}, u32[]{:S(2)}) async-start(f32[16,1,1]{2,1,0:T(1,128)} %broadcast_in_dim.53), calls=%async_computation | async-start | bytes 16384 | tf_op jit(solution)/shard_map/all_to_all | solution.py:87
  19.8 17.5 %copy-start.2 = (f32[1,2,256,256]{3,2,1,0:T(8,128)S(1)}, f32[1,2,256,256]{3,2,1,0:T(8,128)}, u32[]{:S(2)}) copy-start(f32[1,2,256,256]{3,2,1,0:T(8,128)} %param.20) | copy-start | bytes 1572868
  23.9 11.8 %collective-permute-start.2 = (f32[2,384,64]{2,1,0:T(8,128)S(1)}, f32[2,384,64]{2,1,0:T(8,128)S(1)}, u32[]{:S(2)}, u32[]{:S(2)}) collective-permute-start(f32[2,384,64]{2,1,0:T(8,128)S(1)} %get-tuple-element.720), channel_id=1, source_target_pairs={{0,1},{1,2},{2,3},{3,0},{4,5},{5,6},{6,7},{7,4},{8,9},{9,10},{10,1... | collective-permute-start | bytes 589832 | tf_op jit(solution)/shard_map/ppermute | solution.py:17
  27.1 10.1 %collective-permute-start.3 = (f32[2,384,64]{2,1,0:T(8,128)S(1)}, f32[2,384,64]{2,1,0:T(8,128)S(1)}, u32[]{:S(2)}, u32[]{:S(2)}) collective-permute-start(f32[2,384,64]{2,1,0:T(8,128)S(1)} %get-tuple-element.721), channel_id=1, source_target_pairs={{1,0},{2,1},{3,2},{0,3},{5,4},{6,5},{7,6},{4,7},{9,8},{10,9},{11,1... | collective-permute-start | bytes 589832 | tf_op jit(solution)/shard_map/ppermute | solution.py:20
  80.6 103.1 %all-to-all-start.1 = ((f32[16,1,2,128,128]{3,4,2,1,0:T(8,128)}), f32[16,1,2,128,128]{3,4,2,1,0:T(8,128)S(1)}, u32[]{:S(2)}, u32[]{:S(2)}) async-start(f32[16,1,2,128,128]{3,4,2,1,0:T(8,128)} %bitcast.454), calls=%async_computation.1 | async-start | bytes 4194304 | tf_op jit(solution)/shard_map/all_to_all | solution.py:86
  431.1 103.2 %copy-start.1 = (s32[1,1,12,2]{2,3,1,0:T(2,128)S(1)}, s32[1,1,12,2]{2,3,1,0:T(2,128)}, u32[]{:S(2)}) copy-start(s32[1,1,12,2]{2,3,1,0:T(2,128)} %param.23) | copy-start | bytes 292
  431.1 103.1 %all-to-all-start.2 = ((f32[16,1,2,128,128]{3,4,2,1,0:T(8,128)}), f32[16,1,2,128,128]{3,4,2,1,0:T(8,128)S(1)}, u32[]{:S(2)}, u32[]{:S(2)}) async-start(f32[16,1,2,128,128]{3,4,2,1,0:T(8,128)} %bitcast.45), calls=%async_computation.2 | async-start | bytes 4194304 | tf_op jit(solution)/shard_map/all_to_all | solution.py:124
  700.3 8.1 %collective-permute-start.4 = (f32[2,64,384]{2,1,0:T(8,128)S(1)}, f32[2,64,384]{2,1,0:T(8,128)S(1)}, u32[]{:S(2)}, u32[]{:S(2)}) collective-permute-start(f32[2,64,384]{2,1,0:T(8,128)S(1)} %get-tuple-element.717), channel_id=1, source_target_pairs={{0,4},{4,8},{8,12},{12,16},{16,20},{20,24},{24,28},{28,0},{1,5},{5... | collective-permute-start | bytes 589832 | tf_op jit(solution)/shard_map/ppermute | solution.py:17
  705.8 5.1 collective-permute-start.5
  711.1 12.3 %collective-permute-start.6 = (f32[2,256,64]{2,1,0:T(8,128)S(1)}, f32[2,256,64]{2,1,0:T(8,128)S(1)}, u32[]{:S(2)}, u32[]{:S(2)}) collective-permute-start(f32[2,256,64]{2,1,0:T(8,128)S(1)} %get-tuple-element.719), channel_id=1, source_target_pairs={{0,1},{1,2},{2,3},{3,0},{4,5},{5,6},{6,7},{7,4},{8,9},{9,10},{10,1... | collective-permute-start | bytes 393224 | tf_op jit(solution)/shard_map/ppermute | solution.py:17
  716.3 10.1 %collective-permute-start.7 = (f32[2,256,64]{2,1,0:T(8,128)S(1)}, f32[2,256,64]{2,1,0:T(8,128)S(1)}, u32[]{:S(2)}, u32[]{:S(2)}) collective-permute-start(f32[2,256,64]{2,1,0:T(8,128)S(1)} %get-tuple-element.718), channel_id=1, source_target_pairs={{1,0},{2,1},{3,2},{0,3},{5,4},{6,5},{7,6},{4,7},{9,8},{10,9},{11,1... | collective-permute-start | bytes 393224 | tf_op jit(solution)/shard_map/ppermute | solution.py:20
  724.7 1.8 copy-start.3
where the time goes:
time: 732 us; the launch traced here: 728 us
  waiting for transfers between devices  197 us (27%)
  local copies, waits for them, and re-layouts  163 us (22%)
  matrix products  144 us (20%)
  loops' own time  111 us (15%)
  starting transfers between devices  60.4 us (8%)
  other arithmetic  49.5 us (7%)
    all_to_all x1, waiting for transfers between devices, local(): lax.all_to_all(sending, 'depth', split_axis=0, concat_axis=0, tiled=True)  91.9 us
    all_to_all x1, waiting for transfers between devices, local(): lax.all_to_all(outgoing, 'depth', split_axis=0, concat_axis=0, tiled=True)  88 us
    another operation x1, loops' own time, local(): gradient_pad = lax.fori_loop(0, sections * per_device, place, gradient_pad)  86.4 us
    gather x80, local copies, waits for them, and re-layouts  42.6 us
    dynamic_update_slice x16, local copies, waits for them, and re-layouts, place(): lax.dynamic_update_slice(gradient_pad, current + flat_terms[which] * flat...  37.8 us
    dot_general x66, matrix products, transform(): jnp.einsum('psjk,kl->psjl', halfway, cosine_table, precision=HIGHEST)  36.5 us
    dot_general x66, matrix products, transform(): jnp.einsum('psjk,kl->psjl', halfway, imag_table, precision=HIGHEST)  36.4 us
    dot_general x66, matrix products, transform(): jnp.einsum('jk,pskl->psjl', imag_table, planes, precision=HIGHEST)  35.9 us
  transfers between devices with their start and end apart: 11, of which 8 were waited for; matrix products, arithmetic and copies ran while one was open for 7% of the time, Pallas kernels for 0%

commit v1 on v0

v1 whole, which is shorter than its diff:
```python
import functools
import math

import jax
import jax.numpy as jnp
from jax import lax
from jax.experimental import pallas as pl
from jax.experimental.pallas import tpu as pltpu
from jax.sharding import PartitionSpec as P

GROUP = 2
LAG_NUM, LAG_DEN = 9, 5
STAGGER = 1400
MESH = pl.DeviceIdType.MESH
F32 = jnp.float32
BF16 = jnp.bfloat16


def padded_2(block, sides, width):
    for axis, dim in sides:
        count = lax.axis_size(axis)
        forward = [(i, (i + 1) % count) for i in range(count)]
        backward = [(target, source) for source, target in forward]
        low = lax.ppermute(
            lax.slice_in_dim(block, block.shape[dim] - width, None, axis=dim), axis, forward
        )
        high = lax.ppermute(lax.slice_in_dim(block, 0, width, axis=dim), axis, backward)
        block = jnp.concatenate([low, block, high], axis=dim)
    return block


def split(values):
    high = values.astype(BF16)
    return high, (values - high.astype(F32)).astype(BF16)


def times(wave, high_table, low_table):
    high, low = split(wave)
    total = jnp.dot(high, low_table, preferred_element_type=F32)
    total += jnp.dot(low, high_table, preferred_element_type=F32)
    return total + jnp.dot(high, high_table, preferred_element_type=F32)


def turned(wave):
    n = wave.shape[0]
    return jnp.concatenate([wave[:, :n].T, wave[:, n:].T], axis=1)


def both_sides(wave, high_table, low_table):
    return times(turned(times(wave, high_table, low_table)), high_table, low_table)


def multiply(first, second):
    n = first.shape[0]
    a, b, c, d = first[:, :n], first[:, n:], second[:, :n], second[:, n:]
    return jnp.concatenate([a * c - b * d, a * d + b * c], axis=1)


def conj_multiply(first, second):
    n = first.shape[0]
    a, b, c, d = first[:, :n], first[:, n:], second[:, :n], second[:, n:]
    return jnp.concatenate([a * c + b * d, a * d - b * c], axis=1)


def keep_table(real, imag, at, high_ref, low_ref):
    n = real.shape[0]
    (rh, rl), (ih, il) = split(real), split(imag)
    for ref, r, m in ((high_ref, rh, ih), (low_ref, rl, il)):
        ref[at, 0:n, 0:n] = r
        ref[at, 0:n, n : 2 * n] = m
        ref[at, n : 2 * n, 0:n] = -m
        ref[at, n : 2 * n, n : 2 * n] = r


def gather(centers, owners, padded, probes, cuts, starts):
    windows, n = cuts.shape[:2]
    flipped = lax.rem(lax.axis_index("depth"), 2) == 0

    @pl.loop(0, windows)
    def _(w):
        row, col = centers[w, 0], centers[w, 1]
        row_in, col_in = lax.rem(row, 8), lax.rem(col, 128)
        rows = pl.ds(pl.multiple_of(row - row_in, 8), n + 8)
        cols = pl.ds(pl.multiple_of(col - col_in, 128), 2 * n)
        planes = []
        for plane in range(2):
            block = padded[plane, rows, cols]
            block = pltpu.roll(block, lax.rem(2 * n - col_in, 2 * n), 1)[:, :n]
            planes.append(pltpu.roll(block, lax.rem(n + 8 - row_in, n + 8), 0)[:n])

        @pl.when(flipped)
        def _():
            cuts[w] = jnp.concatenate([planes[0].T, planes[1].T], axis=1)

        @pl.when(jnp.logical_not(flipped))
        def _():
            cuts[w] = jnp.concatenate(planes, axis=1)

        probe = probes[owners[w, 0]]
        starts[w] = jnp.concatenate([probe[0], probe[1]], axis=1)


def chain(
    windows, group, groups,
    phase, tables, cut, starts, measured,
    terms,
    phases, forth_high, forth_low, back_high, back_low,
    patches, psis, waves_in, waves_out, turns_in, turns_out, landed,
    phase_sent, phase_got, cut_sent, patch_got, wave_sent, wave_got, turn_sent, turn_got,
    term_sent, term_got,
):
    n = tables.shape[0]
    place = lax.axis_index("depth")
    mine = lax.rem(place, group)
    stage = lax.div(place, group)
    last = groups - 1
    count = lax.div(windows - mine + group - 1, group)

    def send(src, dst, sent, got, target):
        return pltpu.make_async_remote_copy(
            src_ref=src, dst_ref=dst, send_sem=sent, recv_sem=got,
            device_id={"depth": target}, device_id_type=MESH,
        )

    def beside(step):
        return stage * group + lax.rem(mine + step, group)

    barrier = pltpu.get_barrier_semaphore()
    for step in range(1, group):
        pl.semaphore_signal(barrier, inc=1, device_id={"depth": beside(step)}, device_id_type=MESH)

    @pl.when(stage > 0)
    def _():
        pl.semaphore_signal(barrier, inc=1, device_id={"depth": place - group}, device_id_type=MESH)

    @pl.when(stage < last)
    def _():
        pl.semaphore_signal(barrier, inc=1, device_id={"depth": place + group}, device_id_type=MESH)

    inner = jnp.where(stage > 0, 1, 0) + jnp.where(stage < last, 1, 0)
    pl.semaphore_wait(barrier, group - 1 + inner)

    for step in range(1, group):
        send(phase, phases.at[mine], phase_sent.at[step], phase_got.at[mine], beside(step)).start()

    def patch_copy(w):
        which = lax.div(w, group)
        to = lax.rem(w, group)
        return send(
            cut.at[w], patches.at[which, mine], cut_sent.at[w], patch_got.at[which, mine],
            stage * group + to,
        )

    @pl.loop(0, windows)
    def _(w):
        to = lax.rem(w, group)

        @pl.when(to != mine)
        def _():
            patch_copy(w).start()

        @pl.when(to == mine)
        def _():
            patches[lax.div(w, group), mine] = cut[w]

    cosine, sine = tables[:, :n], tables[:, n:]
    keep_table(cosine, -sine, group, forth_high, forth_low)
    keep_table(cosine, sine, group, back_high, back_low)
    phases[mine] = phase[...]
    for step in range(1, group):
        other = lax.rem(mine + step, group)
        send(phase, phases.at[other], phase_sent.at[step], phase_got.at[other], beside(step)).wait_recv()

    @pl.loop(0, group)
    def _(r):
        turn = phases[r]
        real, imag = turn[0:1, :n], turn[0:1, n:]
        scaled = jnp.concatenate([cosine * real - sine * imag, cosine * imag + sine * real], axis=1)
        table = times(scaled, forth_high[group], forth_low[group])
        keep_table(table[:, :n], table[:, n:], r, forth_high, forth_low)
        keep_table(table[:, :n], -table[:, n:], r, back_high, back_low)

    def wave_copy(j):
        return send(waves_out.at[j], waves_in.at[j], wave_sent.at[j], wave_got.at[j], place + group)

    def turn_copy(j):
        return send(turns_out.at[j], turns_in.at[j], turn_sent.at[j], turn_got.at[j], place - group)

    def term_copy(j, r):
        return send(
            psis.at[j, r], landed.at[j * group + mine], term_sent.at[j, r],
            term_got.at[j * group + mine], stage * group + r,
        )

    if STAGGER:
        shared = 2 * mine + lax.rem(lax.axis_index("tx"), 2)
        for turn in range(1, 2 * group):

            @pl.when((stage == 0) & (shared == turn))
            def _():
                pl.delay(turn * STAGGER)

    def go(j):
        @pl.when(stage == 0)
        def _():
            waves_in[j] = starts[j * group + mine]

        @pl.when(stage > 0)
        def _():
            wave_copy(j).wait_recv()

        wave = waves_in[j]
        for r in range(group):
            psi = both_sides(wave, forth_high[r], forth_low[r])
            psis[j, r] = psi

            @pl.when(mine != r)
            def _():
                send(
                    cut.at[0], patches.at[j, r], cut_sent.at[0], patch_got.at[j, r], stage * group + r
                ).wait_recv()

            wave = multiply(psi, patches[j, r])

        @pl.when(stage < last)
        def _():
            waves_out[j] = wave
            wave_copy(j).start()

        @pl.when(stage == last)
        def _():
            far = both_sides(wave, forth_high[group], forth_low[group])
            real, imag = far[:, :n], far[:, n:]
            target = measured[j * group + mine].T
            excess = 2.0 * (real * real + imag * imag - target)
            chi = jnp.concatenate([excess * real, excess * imag], axis=1)
            turns_in[j] = both_sides(chi, back_high[group], back_low[group])

    def come_back(j):
        @pl.when(stage < last)
        def _():
            turn_copy(j).wait_recv()

        wave = turns_in[j]
        for r in reversed(range(group)):
            term = conj_multiply(psis[j, r], wave)
            if r % 2 == 0:
                term = turned(term)

            @pl.when(mine == r)
            def _():
                landed[j * group + mine] = term

            @pl.when(mine != r)
            def _():
                psis[j, r] = term
                term_copy(j, r).start()

            wave = both_sides(conj_multiply(patches[j, r], wave), back_high[r], back_low[r])

        @pl.when(stage > 0)
        def _():
            turns_out[j] = wave
            turn_copy(j).start()

    lag = jnp.minimum(count, lax.div((last - stage) * LAG_NUM, LAG_DEN))

    @pl.loop(0, count + lag)
    def _(t):
        @pl.when(t < count)
        def _():
            go(t)

        @pl.when(t >= lag)
        def _():
            come_back(t - lag)

    for step in range(1, group):
        send(phase, phases.at[mine], phase_sent.at[step], phase_got.at[mine], beside(step)).wait_send()

    @pl.loop(0, windows)
    def _(w):
        @pl.when(lax.rem(w, group) != mine)
        def _():
            patch_copy(w).wait_send()
            send(
                psis.at[0, 0], landed.at[w], term_sent.at[0, 0], term_got.at[w], beside(1)
            ).wait_recv()

    @pl.loop(0, count)
    def _(j):
        @pl.when(stage < last)
        def _():
            wave_copy(j).wait_send()

        @pl.when(stage > 0)
        def _():
            turn_copy(j).wait_send()

        for r in range(group):

            @pl.when(mine != r)
            def _():
                term_copy(j, r).wait_send()

    @pl.loop(0, windows)
    def _(w):
        terms[w] = landed[w]


def spread(centers, terms, total):
    windows, n = terms.shape[0], terms.shape[1]
    total[...] = jnp.zeros(total.shape, F32)

    @pl.loop(0, windows)
    def _(w):
        row, col = centers[w, 0], centers[w, 1]
        row_in, col_in = lax.rem(row, 8), lax.rem(col, 128)
        rows = pl.ds(pl.multiple_of(row - row_in, 8), n + 8)
        cols = pl.ds(pl.multiple_of(col - col_in, 128), 2 * n)
        term = terms[w]
        for plane in range(2):
            block = term[:, plane * n : (plane + 1) * n]
            block = jnp.concatenate([block, jnp.zeros((8, n), F32)], axis=0)
            block = pltpu.roll(block, row_in, 0)
            block = jnp.concatenate([block, jnp.zeros((n + 8, n), F32)], axis=1)
            total[plane, rows, cols] += pltpu.roll(block, col_in, 1)


def local(slices, thickness, probes, centers, batch_of, intensity):
    sections = lax.axis_size("depth")
    n = probes.shape[-1]
    half = n // 2
    centre_table, owners, measured = centers[0, 0], batch_of[0, 0], intensity[0, 0]
    windows = owners.shape[0]
    group, groups = GROUP, sections // GROUP
    most = -(-windows // group)

    padded = padded_2(slices[0], (("tx", 1), ("ty", 2)), half)
    side_rows, side_cols = padded.shape[1:]
    counts = jnp.arange(n, dtype=jnp.int32)
    angles = (counts[:, None] * counts[None, :] % n).astype(F32) * (2.0 * math.pi / n)
    tables = jnp.concatenate([jnp.cos(angles), jnp.sin(angles)], axis=1) * (1.0 / math.sqrt(n))
    offset = (counts + half) % n - half
    turn = thickness[0] * ((offset * offset).astype(F32) * (math.pi / (half * half)))
    phase = jnp.broadcast_to(jnp.concatenate([jnp.cos(turn), -jnp.sin(turn)])[None], (8, 2 * n))

    smem = pl.BlockSpec(memory_space=pltpu.SMEM)
    vmem = pl.BlockSpec(memory_space=pltpu.VMEM)
    page = (n, 2 * n)
    dma = pltpu.SemaphoreType.DMA
    cuts, starts = pl.pallas_call(
        gather,
        name="gather",
        out_shape=[jax.ShapeDtypeStruct((windows, *page), F32)] * 2,
        in_specs=[smem, smem, vmem, vmem],
        out_specs=[vmem, vmem],
    )(centre_table, owners, padded, probes)

    terms = pl.pallas_call(
        functools.partial(chain, windows, group, groups),
        name="chain",
        out_shape=jax.ShapeDtypeStruct((windows, *page), F32),
        in_specs=[vmem, vmem, vmem, vmem, vmem],
        out_specs=vmem,
        scratch_shapes=[
            pltpu.VMEM((group, 8, 2 * n), F32),
            pltpu.VMEM((group + 1, 2 * n, 2 * n), BF16),
            pltpu.VMEM((group + 1, 2 * n, 2 * n), BF16),
            pltpu.VMEM((group + 1, 2 * n, 2 * n), BF16),
            pltpu.VMEM((group + 1, 2 * n, 2 * n), BF16),
            pltpu.VMEM((most, group, *page), F32),
            pltpu.VMEM((most, group, *page), F32),
            pltpu.VMEM((most, *page), F32),
            pltpu.VMEM((most, *page), F32),
            pltpu.VMEM((most, *page), F32),
            pltpu.VMEM((most, *page), F32),
            pltpu.VMEM((windows, *page), F32),
            dma((group,)),
            dma((group,)),
            dma((windows,)),
            dma((most, group)),
            dma((most,)),
            dma((most,)),
            dma((most,)),
            dma((most,)),
            dma((most, group)),
            dma((windows,)),
        ],
        compiler_params=pltpu.CompilerParams(collective_id=0, has_side_effects=True),
    )(phase, tables, cuts, starts, measured)

    gradient_pad = pl.pallas_call(
        spread,
        name="spread",
        out_shape=jax.ShapeDtypeStruct((2, side_rows, side_cols), F32),
        in_specs=[smem, vmem],
        out_specs=vmem,
    )(centre_table, terms)

    row_rims = jnp.concatenate([gradient_pad[:, :half], gradient_pad[:, -half:]], axis=1)
    beside_all = padded_2(row_rims, (("tx", 1),), half)
    inner = gradient_pad[:, half:-half]
    inner = inner.at[:, :half].add(beside_all[:, :half])
    inner = inner.at[:, -half:].add(beside_all[:, -half:])
    col_rims = jnp.concatenate([inner[:, :, :half], inner[:, :, -half:]], axis=2)
    beside = padded_2(col_rims, (("ty", 2),), half)
    result = inner[:, :, half:-half]
    result = result.at[:, :, :half].add(beside[:, :, :half])
    result = result.at[:, :, -half:].add(beside[:, :, -half:])
    return result[None]


def solution(mesh):
    placed = (
        P("depth", None, "tx", "ty"),
        P("depth"),
        P(),
        P("tx", "ty", None, None),
        P("tx", "ty", None, None),
        P("tx", "ty", None, None, None),
    )
    return jax.shard_map(
        local, mesh=mesh, in_specs=placed, out_specs=P("depth", None, "tx", "ty"), check_vma=False
    )
```

time: 732 us -> 251 us (0.34)
  waiting for transfers between devices: 197 us -> 11.6 us
  Pallas kernels: 0 us -> 181 us
  local copies, waits for them, and re-layouts: 163 us -> 9.3 us
  matrix products: 144 us -> 0 us
  loops' own time: 111 us -> 0 us
  other arithmetic: 49.5 us -> 3.92 us
  starting transfers between devices: 60.4 us -> 44 us
    pallas_call x0 -> x3, Pallas kernels: none -> 181 us  [the longest x1 171 us: local(): pl.pallas_call(functools.partial(chain, windows, group, groups), name='ch...]
    all_to_all x3 -> x0, waiting for transfers between devices: 180 us -> none  [the longest x1 91.9 us: local(): lax.all_to_all(sending, 'depth', split_axis=0, concat_axis=0, tiled=True)]
    dot_general x264 -> x0, matrix products: 144 us -> none  [the longest x66 36.5 us: transform(): jnp.einsum('psjk,kl->psjl', halfway, cosine_table, precision=HIGHEST)]
    another operation x4 -> x0, loops' own time: 111 us -> none  [the longest x1 86.4 us: local(): gradient_pad = lax.fori_loop(0, sections * per_device, place, gradient_pad)]
    dynamic_slice x112 -> x0, local copies, waits for them, and re-layouts: 50.7 us -> none  [the longest x32 19.9 us: local(): lax.scan(forward_layer, start_wave, (layers, all_thick[:, 0]))]
    gather x83 -> x0, local copies, waits for them, and re-layouts: 46 us -> none
    dynamic_update_slice x16 -> x0, local copies, waits for them, and re-layouts: 37.8 us -> none  [place(): lax.dynamic_update_slice(gradient_pad, current + flat_terms[which] * flat...]
    all_to_all x3 -> x0, starting transfers between devices: 33 us -> none  [the longest x1 11.2 us: local(): lax.all_to_all(sending, 'depth', split_axis=0, concat_axis=0, tiled=True)]
  transfers between devices with their start and end apart: 11 -> 8, of which waited for: 8 -> 6; matrix products, arithmetic and copies ran while one was open for 7% -> 2% of each run, Pallas kernels for 0% -> 0%
where the time goes in v1:
time: 251 us
  Pallas kernels  181 us (72%)
  starting transfers between devices  44 us (18%)
  waiting for transfers between devices  11.6 us (5%)
  local copies, waits for them, and re-layouts  9.3 us (4%)
  other arithmetic  3.92 us (2%)
    pallas_call x1, Pallas kernels, local(): pl.pallas_call(functools.partial(chain, windows, group, groups), name='ch...  171 us
    ppermute x4, starting transfers between devices, padded_2(): lax.ppermute(lax.slice_in_dim(block, block.shape[dim] - width, None, axis...  27.3 us
    ppermute x4, starting transfers between devices, padded_2(): lax.ppermute(lax.slice_in_dim(block, 0, width, axis=dim), axis, backward)  16.7 us
    ppermute x4, waiting for transfers between devices, padded_2(): lax.ppermute(lax.slice_in_dim(block, block.shape[dim] - width, None, axis...  7.88 us
    pallas_call x1, Pallas kernels, local(): pl.pallas_call(gather, name='gather', out_shape=[jax.ShapeDtypeStruct((wi...  6.38 us
  transfers between devices with their start and end apart: 8, of which 6 were waited for; matrix products, arithmetic and copies ran while one was open for 2% of the time, Pallas kernels for 0%

profile of v1, /device:TPU:1, one launch (start us, length us, event | category | flops | bytes accessed | tf_op | source)
XLA Modules:
  0.0 250.7 jit_solution(4798272210119261100)
XLA Ops:
  0.0 1.0 fusion.20
  1.0 2.6 %collective-permute-start = (f32[2,64,256]{2,1,0:T(8,128)S(1)}, f32[2,64,256]{2,1,0:T(8,128)S(1)}, u32[]{:S(2)}, u32[]{:S(2)}) collective-permute-start(f32[2,64,256]{2,1,0:T(8,128)S(1)} %get-tuple-element.63), channel_id=1, source_target_pairs={{0,4},{4,8},{8,12},{12,16},{16,20},{20,24},{24,28},{28,0},{1,5},{5... | collective-permute-start | bytes 393224 | tf_op jit(solution)/shard_map/ppermute | solution.py:24
  3.6 4.3 %collective-permute-start.1 = (f32[2,64,256]{2,1,0:T(8,128)S(1)}, f32[2,64,256]{2,1,0:T(8,128)S(1)}, u32[]{:S(2)}, u32[]{:S(2)}) collective-permute-start(f32[2,64,256]{2,1,0:T(8,128)S(1)} %get-tuple-element.64), channel_id=1, source_target_pairs={{4,0},{8,4},{12,8},{16,12},{20,16},{24,20},{28,24},{0,28},{5,1},{9... | collective-permute-start | bytes 393224 | tf_op jit(solution)/shard_map/ppermute | solution.py:27
  8.6 1.4 copy.9.centers
  9.9 1.3 copy.8.owners
  11.3 0.3 fusion.9
  11.5 0.0 collective-permute-done
  11.5 0.0 collective-permute-done.1
  11.6 1.1 pad_maximum_fusion.1
  12.7 0.0 copy-start.1
  12.7 0.2 fusion.19
  12.8 1.9 collective-permute-start.2
  14.8 4.6 %collective-permute-start.3 = (f32[2,384,64]{2,1,0:T(8,128)S(1)}, f32[2,384,64]{2,1,0:T(8,128)S(1)}, u32[]{:S(2)}, u32[]{:S(2)}) collective-permute-start(f32[2,384,64]{2,1,0:T(8,128)S(1)} %get-tuple-element.62), channel_id=1, source_target_pairs={{1,0},{2,1},{3,2},{0,3},{5,4},{6,5},{7,6},{4,7},{9,8},{10,9},{11,1... | collective-permute-start | bytes 589832 | tf_op jit(solution)/shard_map/ppermute | solution.py:27
  19.4 0.7 maximum_multiply_fusion.tables
  20.0 3.7 %collective-permute-done.2 = f32[2,384,64]{2,1,0:T(8,128)S(1)} collective-permute-done((f32[2,384,64]{2,1,0:T(8,128)S(1)}, f32[2,384,64]{2,1,0:T(8,128)S(1)}, u32[]{:S(2)}, u32[]{:S(2)}) %collective-permute-start.2) | collective-permute-done | bytes 196640 | tf_op jit(solution)/shard_map/ppermute | solution.py:24
  23.7 0.9 collective-permute-done.3
  24.6 0.0 copy-done.1
  24.6 1.5 pad_maximum_fusion.padded
  26.1 6.4 %gather.1 = (f32[12,128,256]{2,1,0:T(8,128)}, f32[12,128,256]{2,1,0:T(8,128)}) custom-call(s32[12,2]{1,0:T(8,128)} %copy.9.centers, s32[12,1]{1,0:T(8,128)} %copy.8.owners, f32[2,384,384]{2,1,0:T(8,128)} %pad_maximum_fusion.padded, f32[8,2,128,128]{3,2,1,0:T(8,128)} %probes.1), custom_call_target="tpu_custom_call" | custom-call | tf_op jit(solution)/shard_map/gather/pallas_call | solution.py:352
  32.5 0.6 broadcast_in_dim.6.phase
  33.0 170.5 %chain.1.terms = f32[12,128,256]{2,1,0:T(8,128)} custom-call(f32[8,256]{1,0:T(8,128)} %broadcast_in_dim.6.phase, f32[128,256]{1,0:T(8,128)} %maximum_multiply_fusion.tables, f32[12,128,256]{2,1,0:T(8,128)} %get-tuple-element.55.cut, f32[12,128,256]{2,1,0:T(8,128)} %get-tuple-element.56.starts, f32[12,128,128]{2,1,0:T(8,128)} %bitcast.12), custom_call_target="tpu_custom_call" | custom-call | tf_op jit(solution)/shard_map/chain/pallas_call | solution.py:360
  203.6 4.1 %spread.1 = f32[2,384,384]{2,1,0:T(8,128)} custom-call(s32[12,2]{1,0:T(8,128)} %copy.9.centers, f32[12,128,256]{2,1,0:T(8,128)} %chain.1.terms), custom_call_target="tpu_custom_call" | custom-call | tf_op jit(solution)/shard_map/spread/pallas_call | solution.py:393
  207.7 0.0 copy-start
  207.7 0.0 slice-start
  207.7 1.2 fusion.17
  208.9 19.6 %collective-permute-start.4 = (f32[2,64,384]{2,1,0:T(8,128)S(1)}, f32[2,64,384]{2,1,0:T(8,128)S(1)}, u32[]{:S(2)}, u32[]{:S(2)}) collective-permute-start(f32[2,64,384]{2,1,0:T(8,128)S(1)} %get-tuple-element.58), channel_id=1, source_target_pairs={{0,4},{4,8},{8,12},{12,16},{16,20},{20,24},{24,28},{28,0},{1,5},{5... | collective-permute-start | bytes 589832 | tf_op jit(solution)/shard_map/ppermute | solution.py:24
  228.5 0.0 collective-permute-start.5
  228.5 2.6 %collective-permute-done.4 = f32[2,64,384]{2,1,0:T(8,128)S(1)} collective-permute-done((f32[2,64,384]{2,1,0:T(8,128)S(1)}, f32[2,64,384]{2,1,0:T(8,128)S(1)}, u32[]{:S(2)}, u32[]{:S(2)}) %collective-permute-start.4) | collective-permute-done | bytes 196640 | tf_op jit(solution)/shard_map/ppermute | solution.py:24
  231.1 0.0 copy-done
  231.1 0.0 slice-done
  231.1 2.4 collective-permute-done.5
  233.6 0.1 fusion.18
  233.7 3.2 %collective-permute-start.6 = (f32[2,256,64]{2,1,0:T(8,128)S(1)}, f32[2,256,64]{2,1,0:T(8,128)S(1)}, u32[]{:S(2)}, u32[]{:S(2)}) collective-permute-start(f32[2,256,64]{2,1,0:T(8,128)S(1)} %get-tuple-element.60), channel_id=1, source_target_pairs={{0,1},{1,2},{2,3},{3,0},{4,5},{5,6},{6,7},{7,4},{8,9},{9,10},{10,1... | collective-permute-start | bytes 393224 | tf_op jit(solution)/shard_map/ppermute | solution.py:24
  236.9 0.2 slice.151
  237.1 7.9 %collective-permute-start.7 = (f32[2,256,64]{2,1,0:T(8,128)S(1)}, f32[2,256,64]{2,1,0:T(8,128)S(1)}, u32[]{:S(2)}, u32[]{:S(2)}) collective-permute-start(f32[2,256,64]{2,1,0:T(8,128)S(1)} %get-tuple-element.59), channel_id=1, source_target_pairs={{1,0},{2,1},{3,2},{0,3},{5,4},{6,5},{7,6},{4,7},{9,8},{10,9},{11,1... | collective-permute-start | bytes 393224 | tf_op jit(solution)/shard_map/ppermute | solution.py:27
  245.0 1.6 collective-permute-done.6
  246.6 0.1 slice_add_fusion.1
  246.8 1.1 scatter-add.16
  247.9 0.0 copy-start.2
  247.9 0.4 collective-permute-done.7
  248.3 0.1 fusion
  248.5 0.2 copy-done.2
  248.7 2.0 scatter-add.19
  (4 shorter events, 0.1 us)
Async XLA Ops:
  1.0 10.5 %collective-permute-start = (f32[2,64,256]{2,1,0:T(8,128)S(1)}, f32[2,64,256]{2,1,0:T(8,128)S(1)}, u32[]{:S(2)}, u32[]{:S(2)}) collective-permute-start(f32[2,64,256]{2,1,0:T(8,128)S(1)} %get-tuple-element.63), channel_id=1, source_target_pairs={{0,4},{4,8},{8,12},{12,16},{16,20},{20,24},{24,28},{28,0},{1,5},{5... | collective-permute-start | bytes 393224 | tf_op jit(solution)/shard_map/ppermute | solution.py:24
  3.6 8.0 %collective-permute-start.1 = (f32[2,64,256]{2,1,0:T(8,128)S(1)}, f32[2,64,256]{2,1,0:T(8,128)S(1)}, u32[]{:S(2)}, u32[]{:S(2)}) collective-permute-start(f32[2,64,256]{2,1,0:T(8,128)S(1)} %get-tuple-element.64), channel_id=1, source_target_pairs={{4,0},{8,4},{12,8},{16,12},{20,16},{24,20},{28,24},{0,28},{5,1},{9... | collective-permute-start | bytes 393224 | tf_op jit(solution)/shard_map/ppermute | solution.py:27
  12.7 11.9 %copy-start.1 = (f32[1,2,256,256]{3,2,1,0:T(8,128)S(1)}, f32[1,2,256,256]{3,2,1,0:T(8,128)}, u32[]{:S(2)}) copy-start(f32[1,2,256,256]{3,2,1,0:T(8,128)} %param.14) | copy-start | bytes 1572868
  12.8 10.8 %collective-permute-start.2 = (f32[2,384,64]{2,1,0:T(8,128)S(1)}, f32[2,384,64]{2,1,0:T(8,128)S(1)}, u32[]{:S(2)}, u32[]{:S(2)}) collective-permute-start(f32[2,384,64]{2,1,0:T(8,128)S(1)} %get-tuple-element.61), channel_id=1, source_target_pairs={{0,1},{1,2},{2,3},{3,0},{4,5},{5,6},{6,7},{7,4},{8,9},{9,10},{10,1... | collective-permute-start | bytes 589832 | tf_op jit(solution)/shard_map/ppermute | solution.py:24
  14.8 9.8 %collective-permute-start.3 = (f32[2,384,64]{2,1,0:T(8,128)S(1)}, f32[2,384,64]{2,1,0:T(8,128)S(1)}, u32[]{:S(2)}, u32[]{:S(2)}) collective-permute-start(f32[2,384,64]{2,1,0:T(8,128)S(1)} %get-tuple-element.62), channel_id=1, source_target_pairs={{1,0},{2,1},{3,2},{0,3},{5,4},{6,5},{7,6},{4,7},{9,8},{10,9},{11,1... | collective-permute-start | bytes 589832 | tf_op jit(solution)/shard_map/ppermute | solution.py:27
  207.7 23.4 %copy-start = (f32[2,384,384]{2,1,0:T(8,128)S(1)}, f32[2,384,384]{2,1,0:T(8,128)}, u32[]{:S(2)}) copy-start(f32[2,384,384]{2,1,0:T(8,128)} %spread.1) | copy-start | bytes 3538948
  207.7 23.4 %slice-start = ((f32[2,384,384]{2,1,0:T(8,128)}), f32[2,256,384]{2,1,0:T(8,128)S(1)}, s32[]{:S(2)}) async-start(f32[2,384,384]{2,1,0:T(8,128)} %spread.1), calls=%async_computation | async-start | bytes 1572864 | tf_op jit(solution)/shard_map/slice | solution.py:403
  208.9 22.2 %collective-permute-start.4 = (f32[2,64,384]{2,1,0:T(8,128)S(1)}, f32[2,64,384]{2,1,0:T(8,128)S(1)}, u32[]{:S(2)}, u32[]{:S(2)}) collective-permute-start(f32[2,64,384]{2,1,0:T(8,128)S(1)} %get-tuple-element.58), channel_id=1, source_target_pairs={{0,4},{4,8},{8,12},{12,16},{16,20},{20,24},{24,28},{28,0},{1,5},{5... | collective-permute-start | bytes 589832 | tf_op jit(solution)/shard_map/ppermute | solution.py:24
  228.5 5.1 %collective-permute-start.5 = (f32[2,64,384]{2,1,0:T(8,128)S(1)}, f32[2,64,384]{2,1,0:T(8,128)S(1)}, u32[]{:S(2)}, u32[]{:S(2)}) collective-permute-start(f32[2,64,384]{2,1,0:T(8,128)S(1)} %get-tuple-element.57), channel_id=1, source_target_pairs={{4,0},{8,4},{12,8},{16,12},{20,16},{24,20},{28,24},{0,28},{5,1},{9... | collective-permute-start | bytes 589832 | tf_op jit(solution)/shard_map/ppermute | solution.py:27
  233.7 12.9 %collective-permute-start.6 = (f32[2,256,64]{2,1,0:T(8,128)S(1)}, f32[2,256,64]{2,1,0:T(8,128)S(1)}, u32[]{:S(2)}, u32[]{:S(2)}) collective-permute-start(f32[2,256,64]{2,1,0:T(8,128)S(1)} %get-tuple-element.60), channel_id=1, source_target_pairs={{0,1},{1,2},{2,3},{3,0},{4,5},{5,6},{6,7},{7,4},{8,9},{9,10},{10,1... | collective-permute-start | bytes 393224 | tf_op jit(solution)/shard_map/ppermute | solution.py:24
  237.1 11.2 %collective-permute-start.7 = (f32[2,256,64]{2,1,0:T(8,128)S(1)}, f32[2,256,64]{2,1,0:T(8,128)S(1)}, u32[]{:S(2)}, u32[]{:S(2)}) collective-permute-start(f32[2,256,64]{2,1,0:T(8,128)S(1)} %get-tuple-element.59), channel_id=1, source_target_pairs={{1,0},{2,1},{3,2},{0,3},{5,4},{6,5},{7,6},{4,7},{9,8},{10,9},{11,1... | collective-permute-start | bytes 393224 | tf_op jit(solution)/shard_map/ppermute | solution.py:27
  247.9 0.8 copy-start.2

commit v2 on v1

--- a/solution.py
+++ b/solution.py
@@ -9,24 +9,147 @@
 from jax.sharding import PartitionSpec as P
 
 GROUP = 2
-LAG_NUM, LAG_DEN = 9, 5
-STAGGER = 1400
+BASE, HOMES = 0, 1
+LAG = 13
 MESH = pl.DeviceIdType.MESH
 F32 = jnp.float32
 BF16 = jnp.bfloat16
 
 
-def padded_2(block, sides, width):
-    for axis, dim in sides:
-        count = lax.axis_size(axis)
-        forward = [(i, (i + 1) % count) for i in range(count)]
-        backward = [(target, source) for source, target in forward]
-        low = lax.ppermute(
-            lax.slice_in_dim(block, block.shape[dim] - width, None, axis=dim), axis, forward
+SIDES = [(dx, dy) for dx in (-1, 0, 1) for dy in (-1, 0, 1) if dx or dy]
+
+
+def around(dx, dy):
+    tx, ty = lax.axis_size("tx"), lax.axis_size("ty")
+    return {
+        "tx": lax.rem(lax.axis_index("tx") + dx + tx, tx),
+        "ty": lax.rem(lax.axis_index("ty") + dy + ty, ty),
+    }
+
+
+def greet_all():
+    barrier = pltpu.get_barrier_semaphore()
+    for dx, dy in SIDES:
+        pl.semaphore_signal(barrier, inc=1, device_id=around(dx, dy), device_id_type=MESH)
+    pl.semaphore_wait(barrier, len(SIDES))
+
+
+def packed(first, second, upper):
+    n = first.shape[-1]
+    lane = lax.broadcasted_iota(jnp.int32, first.shape, 1)
+    keep = lane >= n // 2 if upper else lane < n // 2
+    return jnp.where(keep, first, pltpu.roll(second, n // 2, 1))
+
+
+def exchange(strips, pages, corners, strips_in, pages_in, corners_in, sent, got):
+    copies = []
+    for k, (dx, dy) in enumerate(SIDES):
+        if dy == 0:
+            src, dst = strips[dx], strips_in.at[(dx + 1) // 2]
+        elif dx == 0:
+            src, dst = pages.at[(dy + 1) // 2], pages_in.at[(dy + 1) // 2]
+        else:
+            at = (dx + 1) + (dy + 1) // 2
+            src, dst = corners.at[at], corners_in.at[at]
+        copies.append(
+            pltpu.make_async_remote_copy(
+                src_ref=src, dst_ref=dst, send_sem=sent.at[k], recv_sem=got.at[k],
+                device_id=around(dx, dy), device_id_type=MESH,
+            )
         )
-        high = lax.ppermute(lax.slice_in_dim(block, 0, width, axis=dim), axis, backward)
-        block = jnp.concatenate([low, block, high], axis=dim)
-    return block
+    return copies
+
+
+def pack_sides(source, rows, columns, pages, corners):
+    for dy in (-1, 1):
+        upper, cols = columns[dy]
+        first, count = rows[0]
+        half = count // 2
+        for plane in range(2):
+            pages[(dy + 1) // 2, plane] = packed(
+                source[plane, first : first + half, cols], source[plane, first + half : first + count, cols], upper
+            )
+        for dx in (-1, 1):
+            first, count = rows[dx]
+            corners[(dx + 1) + (dy + 1) // 2] = packed(
+                source[0, first : first + count, cols], source[1, first : first + count, cols], upper
+            )
+
+
+def enlarge(tile, padded, pages, corners, strips_in, pages_in, corners_in, sent, got):
+    side, n = tile.shape[1], tile.shape[1] // 2
+    half = n // 2
+    greet_all()
+    rows = {-1: (0, half), 0: (0, side), 1: (side - half, half)}
+    columns = {-1: (False, slice(0, n)), 1: (True, slice(side - n, side))}
+    strips = {-1: tile.at[:, pl.ds(0, half), :], 1: tile.at[:, pl.ds(side - half, half), :]}
+    copies = exchange(strips, pages, corners, strips_in, pages_in, corners_in, sent, got)
+    for copy, (dx, dy) in zip(copies, SIDES):
+        if dy == 0:
+            copy.start()
+    pack_sides(tile, rows, columns, pages, corners)
+    for copy, (dx, dy) in zip(copies, SIDES):
+        if dy != 0:
+            copy.start()
+    padded[:, half : half + side, n : n + side] = tile[...]
+    target_rows = {-1: slice(half + side, side + n), 1: slice(0, half)}
+    target_cols = {-1: slice(n + side, 2 * n + side), 1: slice(0, n)}
+    for copy, (dx, dy) in zip(copies, SIDES):
+        copy.wait_recv()
+        if dy == 0:
+            padded[:, target_rows[dx], n : n + side] = strips_in[(dx + 1) // 2]
+        elif dx == 0:
+            for plane in range(2):
+                page = pages_in[(dy + 1) // 2, plane]
+                padded[plane, half : half + n, target_cols[dy]] = page
+                padded[plane, half + n : half + side, target_cols[dy]] = pltpu.roll(page, half, 1)
+        else:
+            corner = corners_in[(dx + 1) + (dy + 1) // 2]
+            padded[0, target_rows[dx], target_cols[dy]] = corner
+            padded[1, target_rows[dx], target_cols[dy]] = pltpu.roll(corner, half, 1)
+    for copy in copies:
+        copy.wait_send()
+
+
+def fold(total, result, pages, corners, strips_in, pages_in, corners_in, sent, got):
+    side, n = result.shape[1], result.shape[1] // 2
+    half = n // 2
+    greet_all()
+    rows = {-1: (0, half), 0: (half, side), 1: (half + side, half)}
+    columns = {-1: (True, slice(0, n)), 1: (False, slice(n + side, 2 * n + side))}
+    mid = pl.ds(n, side)
+    strips = {-1: total.at[:, pl.ds(0, half), mid], 1: total.at[:, pl.ds(half + side, half), mid]}
+    copies = exchange(strips, pages, corners, strips_in, pages_in, corners_in, sent, got)
+    for copy, (dx, dy) in zip(copies, SIDES):
+        if dy == 0:
+            copy.start()
+    pack_sides(total, rows, columns, pages, corners)
+    for copy, (dx, dy) in zip(copies, SIDES):
+        if dy != 0:
+            copy.start()
+    result[...] = total[:, half : half + side, n : n + side]
+    target_rows = {-1: slice(side - half, side), 1: slice(0, half)}
+    target_cols = {-1: slice(side - n, side), 1: slice(0, n)}
+
+    def masked(page, dy):
+        lane = lax.broadcasted_iota(jnp.int32, page.shape, 1)
+        return jnp.where(lane >= half if dy == -1 else lane < half, page, 0.0)
+
+    for copy, (dx, dy) in zip(copies, SIDES):
+        copy.wait_recv()
+        if dy == 0:
+            result[:, target_rows[dx], :] += strips_in[(dx + 1) // 2]
+        elif dx == 0:
+            for plane in range(2):
+                page = pages_in[(dy + 1) // 2, plane]
+                result[plane, 0:n, target_cols[dy]] += masked(page, dy)
+                result[plane, n:side, target_cols[dy]] += masked(pltpu.roll(page, half, 1), dy)
+        else:
+            corner = corners_in[(dx + 1) + (dy + 1) // 2]
+            result[0, target_rows[dx], target_cols[dy]] += masked(corner, dy)
+            result[1, target_rows[dx], target_cols[dy]] += masked(pltpu.roll(corner, half, 1), dy)
+    for copy in copies:
+        copy.wait_send()
 
 
 def split(values):
@@ -78,7 +201,7 @@
 
     @pl.loop(0, windows)
     def _(w):
-        row, col = centers[w, 0], centers[w, 1]
+        row, col = centers[0, 0, w, 0], centers[0, 0, w, 1] + n // 2
         row_in, col_in = lax.rem(row, 8), lax.rem(col, 128)
         rows = pl.ds(pl.multiple_of(row - row_in, 8), n + 8)
         cols = pl.ds(pl.multiple_of(col - col_in, 128), 2 * n)
@@ -96,7 +219,7 @@
         def _():
             cuts[w] = jnp.concatenate(planes, axis=1)
 
-        probe = probes[owners[w, 0]]
+        probe = probes[owners[0, 0, w, 0]]
         starts[w] = jnp.concatenate([probe[0], probe[1]], axis=1)
 
 
@@ -114,7 +237,11 @@
     mine = lax.rem(place, group)
     stage = lax.div(place, group)
     last = groups - 1
-    count = lax.div(windows - mine + group - 1, group)
+    home = mine - BASE
+    active = (home >= 0) & (home < HOMES)
+    count = jnp.where(active, lax.div(windows - home + HOMES - 1, HOMES), 0)
+    before = active & (stage > 0)
+    after = active & (stage < last)
 
     def send(src, dst, sent, got, target):
         return pltpu.make_async_remote_copy(
@@ -129,23 +256,23 @@
     for step in range(1, group):
         pl.semaphore_signal(barrier, inc=1, device_id={"depth": beside(step)}, device_id_type=MESH)
 
-    @pl.when(stage > 0)
+    @pl.when(before)
     def _():
         pl.semaphore_signal(barrier, inc=1, device_id={"depth": place - group}, device_id_type=MESH)
 
-    @pl.when(stage < last)
+    @pl.when(after)
     def _():
         pl.semaphore_signal(barrier, inc=1, device_id={"depth": place + group}, device_id_type=MESH)
 
-    inner = jnp.where(stage > 0, 1, 0) + jnp.where(stage < last, 1, 0)
+    inner = jnp.where(before, 1, 0) + jnp.where(after, 1, 0)
     pl.semaphore_wait(barrier, group - 1 + inner)
 
     for step in range(1, group):
         send(phase, phases.at[mine], phase_sent.at[step], phase_got.at[mine], beside(step)).start()
 
     def patch_copy(w):
-        which = lax.div(w, group)
-        to = lax.rem(w, group)
+        which = lax.div(w, HOMES)
+        to = BASE + lax.rem(w, HOMES)
         return send(
             cut.at[w], patches.at[which, mine], cut_sent.at[w], patch_got.at[which, mine],
             stage * group + to,
@@ -153,7 +280,7 @@
 
     @pl.loop(0, windows)
     def _(w):
-        to = lax.rem(w, group)
+        to = BASE + lax.rem(w, HOMES)
 
         @pl.when(to != mine)
         def _():
@@ -161,7 +288,7 @@
 
         @pl.when(to == mine)
         def _():
-            patches[lax.div(w, group), mine] = cut[w]
+            patches[lax.div(w, HOMES), mine] = cut[w]
 
     cosine, sine = tables[:, :n], tables[:, n:]
     keep_table(cosine, -sine, group, forth_high, forth_low)
@@ -188,22 +315,14 @@
 
     def term_copy(j, r):
         return send(
-            psis.at[j, r], landed.at[j * group + mine], term_sent.at[j, r],
-            term_got.at[j * group + mine], stage * group + r,
+            psis.at[j, r], landed.at[j * HOMES + home], term_sent.at[j, r],
+            term_got.at[j * HOMES + home], stage * group + r,
         )
-
-    if STAGGER:
-        shared = 2 * mine + lax.rem(lax.axis_index("tx"), 2)
-        for turn in range(1, 2 * group):
-
-            @pl.when((stage == 0) & (shared == turn))
-            def _():
-                pl.delay(turn * STAGGER)
 
     def go(j):
         @pl.when(stage == 0)
         def _():
-            waves_in[j] = starts[j * group + mine]
+            waves_in[j] = starts[j * HOMES + home]
 
         @pl.when(stage > 0)
         def _():
@@ -231,7 +350,7 @@
         def _():
             far = both_sides(wave, forth_high[group], forth_low[group])
             real, imag = far[:, :n], far[:, n:]
-            target = measured[j * group + mine].T
+            target = measured[j * HOMES + home].T
             excess = 2.0 * (real * real + imag * imag - target)
             chi = jnp.concatenate([excess * real, excess * imag], axis=1)
             turns_in[j] = both_sides(chi, back_high[group], back_low[group])
@@ -249,21 +368,22 @@
 
             @pl.when(mine == r)
             def _():
-                landed[j * group + mine] = term
+                landed[j * HOMES + home] = term
 
             @pl.when(mine != r)
             def _():
                 psis[j, r] = term
                 term_copy(j, r).start()
 
-            wave = both_sides(conj_multiply(patches[j, r], wave), back_high[r], back_low[r])
+            if r > 0:
+                wave = both_sides(conj_multiply(patches[j, r], wave), back_high[r], back_low[r])
 
         @pl.when(stage > 0)
         def _():
-            turns_out[j] = wave
+            turns_out[j] = both_sides(conj_multiply(patches[j, 0], wave), back_high[0], back_low[0])
             turn_copy(j).start()
 
-    lag = jnp.minimum(count, lax.div((last - stage) * LAG_NUM, LAG_DEN))
+    lag = jnp.minimum(count, lax.div((2 * (last - stage) + 1) * LAG, 7 * HOMES))
 
     @pl.loop(0, count + lag)
     def _(t):
@@ -280,7 +400,7 @@
 
     @pl.loop(0, windows)
     def _(w):
-        @pl.when(lax.rem(w, group) != mine)
+        @pl.when(BASE + lax.rem(w, HOMES) != mine)
         def _():
             patch_copy(w).wait_send()
             send(
@@ -314,7 +434,7 @@
 
     @pl.loop(0, windows)
     def _(w):
-        row, col = centers[w, 0], centers[w, 1]
+        row, col = centers[0, 0, w, 0], centers[0, 0, w, 1] + n // 2
         row_in, col_in = lax.rem(row, 8), lax.rem(col, 128)
         rows = pl.ds(pl.multiple_of(row - row_in, 8), n + 8)
         cols = pl.ds(pl.multiple_of(col - col_in, 128), 2 * n)
@@ -331,13 +451,11 @@
     sections = lax.axis_size("depth")
     n = probes.shape[-1]
     half = n // 2
-    centre_table, owners, measured = centers[0, 0], batch_of[0, 0], intensity[0, 0]
-    windows = owners.shape[0]
+    measured = intensity[0, 0]
+    windows = measured.shape[0]
     group, groups = GROUP, sections // GROUP
-    most = -(-windows // group)
-
-    padded = padded_2(slices[0], (("tx", 1), ("ty", 2)), half)
-    side_rows, side_cols = padded.shape[1:]
+    most = -(-windows // HOMES)
+
     counts = jnp.arange(n, dtype=jnp.int32)
     angles = (counts[:, None] * counts[None, :] % n).astype(F32) * (2.0 * math.pi / n)
     tables = jnp.concatenate([jnp.cos(angles), jnp.sin(angles)], axis=1) * (1.0 / math.sqrt(n))
@@ -349,13 +467,35 @@
     vmem = pl.BlockSpec(memory_space=pltpu.VMEM)
     page = (n, 2 * n)
     dma = pltpu.SemaphoreType.DMA
+    side = slices.shape[2]
+    tile_shape = jax.ShapeDtypeStruct((2, side, side), F32)
+    wide_shape = jax.ShapeDtypeStruct((2, side + n, side + 2 * n), F32)
+    edges = [
+        pltpu.VMEM((2, 2, n, n), F32),
+        pltpu.VMEM((4, half, n), F32),
+        pltpu.VMEM((2, 2, half, side), F32),
+        pltpu.VMEM((2, 2, n, n), F32),
+        pltpu.VMEM((4, half, n), F32),
+        dma((len(SIDES),)),
+        dma((len(SIDES),)),
+    ]
+    padded = pl.pallas_call(
+        enlarge,
+        name="enlarge",
+        out_shape=wide_shape,
+        in_specs=[vmem],
+        out_specs=vmem,
+        scratch_shapes=edges,
+        compiler_params=pltpu.CompilerParams(collective_id=1, has_side_effects=True),
+    )(slices[0])
+
     cuts, starts = pl.pallas_call(
         gather,
         name="gather",
         out_shape=[jax.ShapeDtypeStruct((windows, *page), F32)] * 2,
         in_specs=[smem, smem, vmem, vmem],
         out_specs=[vmem, vmem],
-    )(centre_table, owners, padded, probes)
+    )(centers, batch_of, padded, probes)
 
     terms = pl.pallas_call(
         functools.partial(chain, windows, group, groups),
@@ -390,24 +530,23 @@
         compiler_params=pltpu.CompilerParams(collective_id=0, has_side_effects=True),
     )(phase, tables, cuts, starts, measured)
 
-    gradient_pad = pl.pallas_call(
+    total = pl.pallas_call(
         spread,
         name="spread",
-        out_shape=jax.ShapeDtypeStruct((2, side_rows, side_cols), F32),
+        out_shape=wide_shape,
         in_specs=[smem, vmem],
         out_specs=vmem,
-    )(centre_table, terms)
-
-    row_rims = jnp.concatenate([gradient_pad[:, :half], gradient_pad[:, -half:]], axis=1)
-    beside_all = padded_2(row_rims, (("tx", 1),), half)
-    inner = gradient_pad[:, half:-half]
-    inner = inner.at[:, :half].add(beside_all[:, :half])
-    inner = inner.at[:, -half:].add(beside_all[:, -half:])
-    col_rims = jnp.concatenate([inner[:, :, :half], inner[:, :, -half:]], axis=2)
-    beside = padded_2(col_rims, (("ty", 2),), half)
-    result = inner[:, :, half:-half]
-    result = result.at[:, :, :half].add(beside[:, :, :half])
-    result = result.at[:, :, -half:].add(beside[:, :, -half:])
+    )(centers, terms)
+
+    result = pl.pallas_call(
+        fold,
+        name="fold",
+        out_shape=tile_shape,
+        in_specs=[vmem],
+        out_specs=vmem,
+        scratch_shapes=edges,
+        compiler_params=pltpu.CompilerParams(collective_id=2, has_side_effects=True),
+    )(total)
     return result[None]
 
 

time: 251 us -> 197 us (0.78)
  starting transfers between devices: 44 us -> 0 us
  waiting for transfers between devices: 11.6 us -> 0 us
  Pallas kernels: 181 us -> 190 us
  local copies, waits for them, and re-layouts: 9.3 us -> 4.52 us
  other arithmetic: 3.92 us -> 1 us
    ppermute x8 -> x0, starting transfers between devices: 44 us -> none  [the longest x4 27.3 us: padded_2(): lax.ppermute(lax.slice_in_dim(block, block.shape[dim] - width, None, axis...]
    pallas_call x1 -> x3, Pallas kernels: 4.09 us -> 42.2 us  [the longest x1 20.6 us: local(): pl.pallas_call(fold, name='fold', out_shape=tile_shape, in_specs=[vmem],...]
    pallas_call x1, Pallas kernels: 171 us -> 141 us  [local(): pl.pallas_call(functools.partial(chain, windows, group, groups), name='ch...]
    ppermute x8 -> x0, waiting for transfers between devices: 11.6 us -> none  [the longest x4 7.88 us: padded_2(): lax.ppermute(lax.slice_in_dim(block, block.shape[dim] - width, None, axis...]
    unnamed x6 -> x5, local copies, waits for them, and re-layouts: 0.26 us -> 3.93 us
    scatter-add x2 -> x0, local copies, waits for them, and re-layouts: 3.08 us -> none  [the longest x1 1.96 us: local(): result = result.at[:, :, -half:].add(beside[:, :, -half:])]
    squeeze x2 -> x0, local copies, waits for them, and re-layouts: 2.69 us -> none  [the longest x1 1.36 us: local(): centers[0, 0]]
    slice x7 -> x0, local copies, waits for them, and re-layouts: 2.67 us -> none  [the longest x1 1.19 us: local(): gradient_pad[:, :half]]
  transfers between devices with their start and end apart: 8 -> 0, of which waited for: 6 -> 0; matrix products, arithmetic and copies ran while one was open for 2% -> 0% of each run, Pallas kernels for 0% -> 0%
where the time goes in v2:
time: 197 us; the launch traced here: 196 us
  Pallas kernels  190 us (96%)
  local copies, waits for them, and re-layouts  4.52 us (2%)
    pallas_call x1, Pallas kernels, local(): pl.pallas_call(functools.partial(chain, windows, group, groups), name='ch...  141 us
    pallas_call x1, Pallas kernels, local(): pl.pallas_call(fold, name='fold', out_shape=tile_shape, in_specs=[vmem],...  20.6 us
    pallas_call x1, Pallas kernels, local(): pl.pallas_call(enlarge, name='enlarge', out_shape=wide_shape, in_specs=[v...  17.4 us
    pallas_call x1, Pallas kernels, local(): pl.pallas_call(gather, name='gather', out_shape=[jax.ShapeDtypeStruct((wi...  6.51 us
    pallas_call x1, Pallas kernels, local(): pl.pallas_call(spread, name='spread', out_shape=wide_shape, in_specs=[sme...  4.23 us

profile of v2, /device:TPU:1, one launch (start us, length us, event | category | flops | bytes accessed | tf_op | source)
XLA Modules:
  0.0 196.4 jit_solution(11666514595575694880)
XLA Ops:
  0.0 0.0 copy-start
  0.0 1.4 copy.9.centers
  1.4 17.4 %enlarge.1.padded = f32[2,384,512]{2,1,0:T(8,128)} custom-call(f32[2,256,256]{2,1,0:T(8,128)} %bitcast.6), custom_call_target="tpu_custom_call" | custom-call | tf_op jit(solution)/shard_map/enlarge/pallas_call | solution.py:482
  18.8 0.0 copy-done
  18.8 0.7 copy.8.owners
  19.5 6.5 %gather.1 = (f32[12,128,256]{2,1,0:T(8,128)}, f32[12,128,256]{2,1,0:T(8,128)}) custom-call(s32[1,1,12,2]{3,2,1,0:T(8,128)} %copy.9.centers, s32[1,1,12,1]{3,2,1,0:T(8,128)} %copy.8.owners, f32[2,384,512]{2,1,0:T(8,128)} %enlarge.1.padded, f32[8,2,128,128]{3,2,1,0:T(8,128)} %probes.1), custom_call_target="tpu_custom_call" | custom-call | tf_op jit(solution)/shard_map/gather/pallas_call | solution.py:492
  26.0 0.3 fusion.6
  26.3 0.7 maximum_multiply_fusion.tables
  27.7 0.6 broadcast_in_dim.4.phase
  28.3 141.4 %chain.1.terms = f32[12,128,256]{2,1,0:T(8,128)} custom-call(f32[8,256]{1,0:T(8,128)} %broadcast_in_dim.4.phase, f32[128,256]{1,0:T(8,128)} %maximum_multiply_fusion.tables, f32[12,128,256]{2,1,0:T(8,128)} %get-tuple-element.7.cut, f32[12,128,256]{2,1,0:T(8,128)} %get-tuple-element.8.starts, f32[12,128,128]{2,1,0:T(8,128)} %bitcast.5), custom_call_target="tpu_custom_call" | custom-call | tf_op jit(solution)/shard_map/chain/pallas_call | solution.py:500
  169.7 4.2 %spread.1.total = f32[2,384,512]{2,1,0:T(8,128)} custom-call(s32[1,1,12,2]{3,2,1,0:T(8,128)} %copy.9.centers, f32[12,128,256]{2,1,0:T(8,128)} %chain.1.terms), custom_call_target="tpu_custom_call" | custom-call | tf_op jit(solution)/shard_map/spread/pallas_call | solution.py:533
  173.9 20.6 %fold.1 = f32[2,256,256]{2,1,0:T(8,128)} custom-call(f32[2,384,512]{2,1,0:T(8,128)} %spread.1.total), custom_call_target="tpu_custom_call" | custom-call | tf_op jit(solution)/shard_map/fold/pallas_call | solution.py:541
  194.5 1.9 copy.12
  (2 shorter events, 0.1 us)
Async XLA Ops:
  0.0 18.8 %copy-start = (s32[1,1,12,1]{2,3,1,0:T(1,128)S(1)}, s32[1,1,12,1]{2,3,1,0:T(1,128)}, u32[]{:S(2)}) copy-start(s32[1,1,12,1]{2,3,1,0:T(1,128)} %param.10) | copy-start | bytes 148

commit v3 on v2

v3 whole, which is shorter than its diff:
```python
import functools
import math

import jax
import jax.numpy as jnp
from jax import lax
from jax.experimental import pallas as pl
from jax.experimental.pallas import tpu as pltpu
from jax.sharding import PartitionSpec as P

LAG = 13
MESH = pl.DeviceIdType.MESH
F32 = jnp.float32
BF16 = jnp.bfloat16


SIDES = [(dx, dy) for dx in (-1, 0, 1) for dy in (-1, 0, 1) if dx or dy]


def around(dx, dy):
    tx, ty = lax.axis_size("tx"), lax.axis_size("ty")
    return {
        "tx": lax.rem(lax.axis_index("tx") + dx + tx, tx),
        "ty": lax.rem(lax.axis_index("ty") + dy + ty, ty),
    }


def greet_all(more=0):
    barrier = pltpu.get_barrier_semaphore()
    for dx, dy in SIDES:
        pl.semaphore_signal(barrier, inc=1, device_id=around(dx, dy), device_id_type=MESH)
    pl.semaphore_wait(barrier, len(SIDES) + more)


def packed(first, second, upper):
    n = first.shape[-1]
    lane = lax.broadcasted_iota(jnp.int32, first.shape, 1)
    keep = lane >= n // 2 if upper else lane < n // 2
    return jnp.where(keep, first, pltpu.roll(second, n // 2, 1))


def exchange(strips, pages, corners, strips_in, pages_in, corners_in, sent, got):
    copies = []
    for k, (dx, dy) in enumerate(SIDES):
        if dy == 0:
            src, dst = strips[dx], strips_in.at[(dx + 1) // 2]
        elif dx == 0:
            src, dst = pages.at[(dy + 1) // 2], pages_in.at[(dy + 1) // 2]
        else:
            at = (dx + 1) + (dy + 1) // 2
            src, dst = corners.at[at], corners_in.at[at]
        copies.append(
            pltpu.make_async_remote_copy(
                src_ref=src, dst_ref=dst, send_sem=sent.at[k], recv_sem=got.at[k],
                device_id=around(dx, dy), device_id_type=MESH,
            )
        )
    return copies


def pack_sides(source, rows, columns, pages, corners):
    for dy in (-1, 1):
        upper, cols = columns[dy]
        first, count = rows[0]
        half = count // 2
        for plane in range(2):
            pages[(dy + 1) // 2, plane] = packed(
                source[plane, first : first + half, cols], source[plane, first + half : first + count, cols], upper
            )
        for dx in (-1, 1):
            first, count = rows[dx]
            corners[(dx + 1) + (dy + 1) // 2] = packed(
                source[0, first : first + count, cols], source[1, first : first + count, cols], upper
            )


def enlarge(
    tile, phase, padded, phases, pages, corners, strips_in, pages_in, corners_in, sent, got, phase_in, phase_sems
):
    side, n = tile.shape[1], tile.shape[1] // 2
    half = n // 2
    place = lax.axis_index("depth")
    mine = lax.rem(place, 2)
    partner = {"depth": place + 1 - 2 * mine}
    pl.semaphore_signal(pltpu.get_barrier_semaphore(), inc=1, device_id=partner, device_id_type=MESH)
    greet_all(1)
    rows = {-1: (0, half), 0: (0, side), 1: (side - half, half)}
    columns = {-1: (False, slice(0, n)), 1: (True, slice(side - n, side))}
    strips = {-1: tile.at[:, pl.ds(0, half), :], 1: tile.at[:, pl.ds(side - half, half), :]}
    copies = exchange(strips, pages, corners, strips_in, pages_in, corners_in, sent, got)
    for copy, (dx, dy) in zip(copies, SIDES):
        if dy == 0:
            copy.start()
    swap = pltpu.make_async_remote_copy(
        src_ref=phase, dst_ref=phase_in, send_sem=phase_sems.at[0], recv_sem=phase_sems.at[1],
        device_id=partner, device_id_type=MESH,
    )
    swap.start()
    pack_sides(tile, rows, columns, pages, corners)
    for copy, (dx, dy) in zip(copies, SIDES):
        if dy != 0:
            copy.start()
    padded[:, half : half + side, n : n + side] = tile[...]
    target_rows = {-1: slice(half + side, side + n), 1: slice(0, half)}
    target_cols = {-1: slice(n + side, 2 * n + side), 1: slice(0, n)}
    for copy, (dx, dy) in zip(copies, SIDES):
        copy.wait_recv()
        if dy == 0:
            padded[:, target_rows[dx], n : n + side] = strips_in[(dx + 1) // 2]
        elif dx == 0:
            for plane in range(2):
                page = pages_in[(dy + 1) // 2, plane]
                padded[plane, half : half + n, target_cols[dy]] = page
                padded[plane, half + n : half + side, target_cols[dy]] = pltpu.roll(page, half, 1)
        else:
            corner = corners_in[(dx + 1) + (dy + 1) // 2]
            padded[0, target_rows[dx], target_cols[dy]] = corner
            padded[1, target_rows[dx], target_cols[dy]] = pltpu.roll(corner, half, 1)
    swap.wait_recv()
    phases[mine] = phase[...]
    phases[1 - mine] = phase_in[...]
    swap.wait_send()
    for copy in copies:
        copy.wait_send()


def fold(total, result, pages, corners, strips_in, pages_in, corners_in, sent, got):
    side, n = result.shape[1], result.shape[1] // 2
    half = n // 2
    greet_all()
    rows = {-1: (0, half), 0: (half, side), 1: (half + side, half)}
    columns = {-1: (True, slice(0, n)), 1: (False, slice(n + side, 2 * n + side))}
    mid = pl.ds(n, side)
    strips = {-1: total.at[:, pl.ds(0, half), mid], 1: total.at[:, pl.ds(half + side, half), mid]}
    copies = exchange(strips, pages, corners, strips_in, pages_in, corners_in, sent, got)
    for copy, (dx, dy) in zip(copies, SIDES):
        if dy == 0:
            copy.start()
    pack_sides(total, rows, columns, pages, corners)
    for copy, (dx, dy) in zip(copies, SIDES):
        if dy != 0:
            copy.start()
    result[...] = total[:, half : half + side, n : n + side]
    target_rows = {-1: slice(side - half, side), 1: slice(0, half)}
    target_cols = {-1: slice(side - n, side), 1: slice(0, n)}

    def masked(page, dy):
        lane = lax.broadcasted_iota(jnp.int32, page.shape, 1)
        return jnp.where(lane >= half if dy == -1 else lane < half, page, 0.0)

    for copy, (dx, dy) in zip(copies, SIDES):
        copy.wait_recv()
        if dy == 0:
            result[:, target_rows[dx], :] += strips_in[(dx + 1) // 2]
        elif dx == 0:
            for plane in range(2):
                page = pages_in[(dy + 1) // 2, plane]
                result[plane, 0:n, target_cols[dy]] += masked(page, dy)
                result[plane, n:side, target_cols[dy]] += masked(pltpu.roll(page, half, 1), dy)
        else:
            corner = corners_in[(dx + 1) + (dy + 1) // 2]
            result[0, target_rows[dx], target_cols[dy]] += masked(corner, dy)
            result[1, target_rows[dx], target_cols[dy]] += masked(pltpu.roll(corner, half, 1), dy)
    for copy in copies:
        copy.wait_send()


def split(values):
    high = values.astype(BF16)
    return high, (values - high.astype(F32)).astype(BF16)


def times(wave, high_table, low_table):
    high, low = split(wave)
    total = jnp.dot(high, low_table, preferred_element_type=F32)
    total += jnp.dot(low, high_table, preferred_element_type=F32)
    return total + jnp.dot(high, high_table, preferred_element_type=F32)


def turned(wave):
    n = wave.shape[0]
    return jnp.concatenate([wave[:, :n].T, wave[:, n:].T], axis=1)


def both_sides(wave, high_table, low_table):
    return times(turned(times(wave, high_table, low_table)), high_table, low_table)


def multiply(first, second):
    n = first.shape[0]
    a, b, c, d = first[:, :n], first[:, n:], second[:, :n], second[:, n:]
    return jnp.concatenate([a * c - b * d, a * d + b * c], axis=1)


def conj_multiply(first, second):
    n = first.shape[0]
    a, b, c, d = first[:, :n], first[:, n:], second[:, :n], second[:, n:]
    return jnp.concatenate([a * c + b * d, a * d - b * c], axis=1)


def keep_table(real, imag, at, high_ref, low_ref):
    n = real.shape[0]
    (rh, rl), (ih, il) = split(real), split(imag)
    for ref, r, m in ((high_ref, rh, ih), (low_ref, rl, il)):
        ref[at, 0:n, 0:n] = r
        ref[at, 0:n, n : 2 * n] = m
        ref[at, n : 2 * n, 0:n] = -m
        ref[at, n : 2 * n, n : 2 * n] = r


def gather(centers, owners, padded, probes, cuts, starts):
    windows, n = cuts.shape[:2]
    flipped = lax.rem(lax.axis_index("depth"), 2) == 0

    @pl.loop(0, windows)
    def _(w):
        row, col = centers[0, 0, 0, w], centers[0, 0, 1, w] + n // 2
        row_in, col_in = lax.rem(row, 8), lax.rem(col, 128)
        rows = pl.ds(pl.multiple_of(row - row_in, 8), n + 8)
        cols = pl.ds(pl.multiple_of(col - col_in, 128), 2 * n)
        planes = []
        for plane in range(2):
            block = padded[plane, rows, cols]
            block = pltpu.roll(block, lax.rem(2 * n - col_in, 2 * n), 1)[:, :n]
            planes.append(pltpu.roll(block, lax.rem(n + 8 - row_in, n + 8), 0)[:n])

        @pl.when(flipped)
        def _():
            cuts[w] = jnp.concatenate([planes[0].T, planes[1].T], axis=1)

        @pl.when(jnp.logical_not(flipped))
        def _():
            cuts[w] = jnp.concatenate(planes, axis=1)

        probe = probes[owners[0, 0, 0, w]]
        starts[w] = jnp.concatenate([probe[0], probe[1]], axis=1)


def chain(
    windows, stages,
    phases, tables, cut, starts, measured,
    terms,
    forth_high, forth_low, back_high, back_low,
    other, psis, turned_terms, waves_in, waves_out, turns_in, turns_out,
    patch_sent, patch_got, wave_sent, wave_got, turn_sent, turn_got, term_sent, term_got,
):
    n = tables.shape[0]
    place = lax.axis_index("depth")
    home = lax.rem(place, 2) == 0
    stage = lax.div(place, 2)
    last = stages - 1
    partner = jnp.where(home, place + 1, place - 1)
    before = home & (stage > 0)
    after = home & (stage < last)

    def copy(src, dst, sent, got, target):
        return pltpu.make_async_remote_copy(
            src_ref=src, dst_ref=dst, send_sem=sent, recv_sem=got,
            device_id={"depth": target}, device_id_type=MESH,
        )

    def patch_copy(w):
        return copy(cut.at[w], other.at[w], patch_sent.at[w], patch_got.at[w], partner)

    def wave_copy(j):
        return copy(waves_out.at[j], waves_in.at[j], wave_sent.at[j], wave_got.at[j], place + 2)

    def turn_copy(j):
        return copy(turns_out.at[j], turns_in.at[j], turn_sent.at[j], turn_got.at[j], place - 2)

    def term_copy(j):
        return copy(turned_terms.at[j], terms.at[j], term_sent.at[j], term_got.at[j], partner)

    barrier = pltpu.get_barrier_semaphore()
    pl.semaphore_signal(barrier, inc=1, device_id={"depth": partner}, device_id_type=MESH)

    @pl.when(before)
    def _():
        pl.semaphore_signal(barrier, inc=1, device_id={"depth": place - 2}, device_id_type=MESH)

    @pl.when(after)
    def _():
        pl.semaphore_signal(barrier, inc=1, device_id={"depth": place + 2}, device_id_type=MESH)

    pl.semaphore_wait(barrier, 1 + jnp.where(before, 1, 0) + jnp.where(after, 1, 0))

    @pl.when(jnp.logical_not(home))
    def _():
        @pl.loop(0, windows)
        def _(w):
            patch_copy(w).start()

    @pl.when(home)
    def _():
        cosine, sine = tables[:, :n], tables[:, n:]
        keep_table(cosine, -sine, 2, forth_high, forth_low)
        keep_table(cosine, sine, 2, back_high, back_low)
        for r in range(2):
            real, imag = phases[r, 0:1, :n], phases[r, 0:1, n:]
            scaled = jnp.concatenate([cosine * real - sine * imag, cosine * imag + sine * real], axis=1)
            table = times(scaled, forth_high[2], forth_low[2])
            keep_table(table[:, :n], table[:, n:], r, forth_high, forth_low)
            keep_table(table[:, :n], -table[:, n:], r, back_high, back_low)

    def forth(wave, at):
        return both_sides(wave, forth_high[at], forth_low[at])

    def back(wave, at):
        return both_sides(wave, back_high[at], back_low[at])

    def through(j):
        first = forth(waves_in[j], 0)
        psis[0, j] = first
        second = forth(multiply(first, cut[j]), 1)
        psis[1, j] = second
        return multiply(second, other[j])

    def detect(j, wave):
        far = forth(wave, 2)
        real, imag = far[:, :n], far[:, n:]
        excess = 2.0 * (real * real + imag * imag - measured[j].T)
        turns_in[j] = back(jnp.concatenate([excess * real, excess * imag], axis=1), 2)

    def second_term(j):
        turned_terms[j] = conj_multiply(psis[1, j], turns_in[j])

    def first_back(j):
        return back(conj_multiply(other[j], turns_in[j]), 1)

    def first_term(j, wave):
        terms[j] = turned(conj_multiply(psis[0, j], wave))

    def second_back(j, wave):
        turns_out[j] = back(conj_multiply(cut[j], wave), 0)

    @pl.when(after)
    def _():
        lag = jnp.minimum(windows, lax.div((2 * (last - stage) + 1) * LAG, 7))

        @pl.loop(0, windows + lag)
        def _(t):
            @pl.when(t < windows)
            def _():
                patch_copy(t).wait_recv()

                @pl.when(stage == 0)
                def _():
                    waves_in[t] = starts[t]

                @pl.when(stage > 0)
                def _():
                    wave_copy(t).wait_recv()

                waves_out[t] = through(t)
                wave_copy(t).start()

            @pl.when(t >= lag)
            def _():
                j = t - lag
                turn_copy(j).wait_recv()

                @pl.when(stage == 0)
                def _():
                    second_term(j)
                    term_copy(j).start()
                    first_term(j, first_back(j))

                @pl.when(stage > 0)
                def _():
                    wave = first_back(j)
                    second_back(j, wave)
                    turn_copy(j).start()
                    second_term(j)
                    first_term(j, wave)

                    @pl.when(t >= windows)
                    def _():
                        term_copy(j).start()

        @pl.when(stage > 0)
        def _():
            @pl.loop(0, windows - lag)
            def _(j):
                term_copy(j).start()

    @pl.when(home & (stage == last))
    def _():
        def arrive(t):
            patch_copy(t).wait_recv()
            wave_copy(t).wait_recv()

        def leave(t):
            turn_copy(t).start()
            term_copy(t).start()

        def finish(t):
            wave = first_back(t)
            second_term(t)
            second_back(t, wave)
            first_term(t, wave)

        arrive(0)
        detect(0, through(0))

        @pl.loop(1, windows)
        def _(t):
            arrive(t)
            finish(t - 1)
            detect(t, through(t))
            leave(t - 1)

        finish(windows - 1)
        leave(windows - 1)

    @pl.when(home)
    def _():
        @pl.loop(0, windows)
        def _(j):
            @pl.when(stage < last)
            def _():
                wave_copy(j).wait_send()

            @pl.when(stage > 0)
            def _():
                turn_copy(j).wait_send()

            term_copy(j).wait_send()

    @pl.when(jnp.logical_not(home))
    def _():
        @pl.loop(0, windows)
        def _(j):
            patch_copy(j).wait_send()
            term_copy(j).wait_recv()


def spread(centers, terms, total):
    windows, n = terms.shape[0], terms.shape[1]
    total[...] = jnp.zeros(total.shape, F32)

    @pl.loop(0, windows)
    def _(w):
        row, col = centers[0, 0, 0, w], centers[0, 0, 1, w] + n // 2
        row_in, col_in = lax.rem(row, 8), lax.rem(col, 128)
        rows = pl.ds(pl.multiple_of(row - row_in, 8), n + 8)
        cols = pl.ds(pl.multiple_of(col - col_in, 128), 2 * n)
        term = terms[w]
        for plane in range(2):
            block = term[:, plane * n : (plane + 1) * n]
            block = jnp.concatenate([block, jnp.zeros((8, n), F32)], axis=0)
            block = pltpu.roll(block, row_in, 0)
            block = jnp.concatenate([block, jnp.zeros((n + 8, n), F32)], axis=1)
            total[plane, rows, cols] += pltpu.roll(block, col_in, 1)


def local(slices, thickness, probes, centers, batch_of, intensity):
    sections = lax.axis_size("depth")
    n = probes.shape[-1]
    half = n // 2
    measured = intensity[0, 0]
    windows = measured.shape[0]
    places = jnp.transpose(centers, (0, 1, 3, 2))
    owners = jnp.transpose(batch_of, (0, 1, 3, 2))
    counts = jnp.arange(n, dtype=jnp.int32)
    angles = (counts[:, None] * counts[None, :] % n).astype(F32) * (2.0 * math.pi / n)
    tables = jnp.concatenate([jnp.cos(angles), jnp.sin(angles)], axis=1) * (1.0 / math.sqrt(n))
    offset = (counts + half) % n - half
    turn = thickness[0] * ((offset * offset).astype(F32) * (math.pi / (half * half)))
    turn = jnp.broadcast_to(turn[None], (8, n))
    phase = jnp.concatenate([jnp.cos(turn), -jnp.sin(turn)], axis=1)

    smem = pl.BlockSpec(memory_space=pltpu.SMEM)
    vmem = pl.BlockSpec(memory_space=pltpu.VMEM)
    page = (n, 2 * n)
    dma = pltpu.SemaphoreType.DMA
    side = slices.shape[2]
    tile_shape = jax.ShapeDtypeStruct((2, side, side), F32)
    wide_shape = jax.ShapeDtypeStruct((2, side + n, side + 2 * n), F32)
    edges = [
        pltpu.VMEM((2, 2, n, n), F32),
        pltpu.VMEM((4, half, n), F32),
        pltpu.VMEM((2, 2, half, side), F32),
        pltpu.VMEM((2, 2, n, n), F32),
        pltpu.VMEM((4, half, n), F32),
        dma((len(SIDES),)),
        dma((len(SIDES),)),
    ]
    padded, phases = pl.pallas_call(
        enlarge,
        name="enlarge",
        out_shape=[wide_shape, jax.ShapeDtypeStruct((2, 8, 2 * n), F32)],
        in_specs=[vmem, vmem],
        out_specs=[vmem, vmem],
        scratch_shapes=[*edges, pltpu.VMEM((8, 2 * n), F32), dma((2,))],
        compiler_params=pltpu.CompilerParams(collective_id=1, has_side_effects=True),
    )(slices[0], phase)

    cuts, starts = pl.pallas_call(
        gather,
        name="gather",
        out_shape=[jax.ShapeDtypeStruct((windows, *page), F32)] * 2,
        in_specs=[smem, smem, vmem, vmem],
        out_specs=[vmem, vmem],
    )(places, owners, padded, probes)

    terms = pl.pallas_call(
        functools.partial(chain, windows, sections // 2),
        name="chain",
        out_shape=jax.ShapeDtypeStruct((windows, *page), F32),
        in_specs=[vmem] * 5,
        out_specs=vmem,
        scratch_shapes=[pltpu.VMEM((3, 2 * n, 2 * n), BF16)] * 4
        + [pltpu.VMEM((windows, *page), F32), pltpu.VMEM((2, windows, *page), F32)]
        + [pltpu.VMEM((windows, *page), F32)] * 5
        + [dma((windows,))] * 8,
        compiler_params=pltpu.CompilerParams(collective_id=0, has_side_effects=True),
    )(phases, tables, cuts, starts, measured)

    total = pl.pallas_call(
        spread,
        name="spread",
        out_shape=wide_shape,
        in_specs=[smem, vmem],
        out_specs=vmem,
    )(places, terms)

    result = pl.pallas_call(
        fold,
        name="fold",
        out_shape=tile_shape,
        in_specs=[vmem],
        out_specs=vmem,
        scratch_shapes=edges,
        compiler_params=pltpu.CompilerParams(collective_id=2, has_side_effects=True),
    )(total)
    return result[None]


def solution(mesh):
    placed = (
        P("depth", None, "tx", "ty"),
        P("depth"),
        P(),
        P("tx", "ty", None, None),
        P("tx", "ty", None, None),
        P("tx", "ty", None, None, None),
    )
    return jax.shard_map(
        local, mesh=mesh, in_specs=placed, out_specs=P("depth", None, "tx", "ty"), check_vma=False
    )
```

time: 197 us -> 179 us (0.909)
  Pallas kernels: 190 us -> 174 us
  local copies, waits for them, and re-layouts: 4.52 us -> 2.47 us
    pallas_call x2, Pallas kernels: 159 us -> 145 us  [the longest x1 127 us: local(): pl.pallas_call(functools.partial(chain, windows, sections // 2), name='ch...]
    unnamed x5 -> x1, local copies, waits for them, and re-layouts: 3.93 us -> 1.87 us
where the time goes in v3:
time: 179 us; the launch traced here: 178 us
  Pallas kernels  174 us (97%)
  local copies, waits for them, and re-layouts  2.47 us (1%)
    pallas_call x1, Pallas kernels, local(): pl.pallas_call(functools.partial(chain, windows, sections // 2), name='ch...  127 us
    pallas_call x1, Pallas kernels, local(): pl.pallas_call(fold, name='fold', out_shape=tile_shape, in_specs=[vmem],...  18.8 us
    pallas_call x1, Pallas kernels, local(): pl.pallas_call(enlarge, name='enlarge', out_shape=[wide_shape, jax.ShapeD...  17.5 us
    pallas_call x1, Pallas kernels, local(): pl.pallas_call(gather, name='gather', out_shape=[jax.ShapeDtypeStruct((wi...  6.52 us
    pallas_call x1, Pallas kernels, local(): pl.pallas_call(spread, name='spread', out_shape=wide_shape, in_specs=[sme...  4.23 us

profile of v3, /device:TPU:1, one launch (start us, length us, event | category | flops | bytes accessed | tf_op | source)
XLA Modules:
  0.0 178.5 jit_solution(15244236356705497119)
XLA Ops:
  0.7 0.6 broadcast.59.phase
  1.3 17.5 %enlarge.1 = (f32[2,384,512]{2,1,0:T(8,128)}, f32[2,8,256]{2,1,0:T(8,128)}) custom-call(f32[2,256,256]{2,1,0:T(8,128)} %bitcast.8, f32[8,256]{1,0:T(8,128)} %broadcast.59.phase), custom_call_target="tpu_custom_call" | custom-call | tf_op jit(solution)/shard_map/enlarge/pallas_call | solution.py:488
  18.8 6.5 %gather.1 = (f32[12,128,256]{2,1,0:T(8,128)}, f32[12,128,256]{2,1,0:T(8,128)}) custom-call(s32[1,1,2,12]{3,2,1,0:T(2,128)} %bitcast.9, s32[1,1,1,12]{3,2,1,0:T(1,128)} %bitcast.11, f32[2,384,512]{2,1,0:T(8,128)} %get-tuple-element.10.padded, f32[8,2,128,128]{3,2,1,0:T(8,128)} %probes.1), custom_call_target="tpu_custom_call" | custom-call | tf_op jit(solution)/shard_map/gather/pallas_call | solution.py:498
  25.3 0.3 fusion.6
  25.6 0.7 maximum_multiply_fusion.tables
  26.3 127.4 %chain.1.terms = f32[12,128,256]{2,1,0:T(8,128)} custom-call(f32[2,8,256]{2,1,0:T(8,128)} %get-tuple-element.9.phases, f32[128,256]{1,0:T(8,128)} %maximum_multiply_fusion.tables, f32[12,128,256]{2,1,0:T(8,128)} %get-tuple-element.11.cut, f32[12,128,256]{2,1,0:T(8,128)} %get-tuple-element.12.starts, f32[12,128,128]{2,1,0:T(8,128)} %bitcast.7), custom_call_target="tpu_custom_call" | custom-call | tf_op jit(solution)/shard_map/chain/pallas_call | solution.py:506
  153.6 4.2 %spread.1.total = f32[2,384,512]{2,1,0:T(8,128)} custom-call(s32[1,1,2,12]{3,2,1,0:T(2,128)} %bitcast.10, f32[12,128,256]{2,1,0:T(8,128)} %chain.1.terms), custom_call_target="tpu_custom_call" | custom-call | tf_op jit(solution)/shard_map/spread/pallas_call | solution.py:519
  157.9 18.8 %fold.1 = f32[2,256,256]{2,1,0:T(8,128)} custom-call(f32[2,384,512]{2,1,0:T(8,128)} %spread.1.total), custom_call_target="tpu_custom_call" | custom-call | tf_op jit(solution)/shard_map/fold/pallas_call | solution.py:527
  176.6 1.9 %copy.9 = f32[1,2,256,256]{3,2,1,0:T(8,128)} copy(f32[1,2,256,256]{3,2,1,0:T(8,128)} %bitcast.6) | data formatting | bytes 1048576
  (2 shorter events, 0.1 us)

commit v4 on v3

--- a/solution.py
+++ b/solution.py
@@ -208,32 +208,31 @@
         ref[at, n : 2 * n, n : 2 * n] = r
 
 
-def gather(centers, owners, padded, probes, cuts, starts):
-    windows, n = cuts.shape[:2]
+def gather(places, owners, padded, first_probe, second_probe, cuts, starts):
+    n = cuts.shape[1]
     flipped = lax.rem(lax.axis_index("depth"), 2) == 0
-
-    @pl.loop(0, windows)
-    def _(w):
-        row, col = centers[0, 0, 0, w], centers[0, 0, 1, w] + n // 2
-        row_in, col_in = lax.rem(row, 8), lax.rem(col, 128)
+    patches = []
+    for k in range(2):
+        w = 2 * pl.program_id(0) + k
+        row, col = places[0, w], places[1, w] + n // 2
+        row_in, col_in = lax.rem(row, 8), lax.rem(col, n)
         rows = pl.ds(pl.multiple_of(row - row_in, 8), n + 8)
-        cols = pl.ds(pl.multiple_of(col - col_in, 128), 2 * n)
-        planes = []
+        cols = pl.ds(pl.multiple_of(col - col_in, n), 2 * n)
         for plane in range(2):
-            block = padded[plane, rows, cols]
-            block = pltpu.roll(block, lax.rem(2 * n - col_in, 2 * n), 1)[:, :n]
-            planes.append(pltpu.roll(block, lax.rem(n + 8 - row_in, n + 8), 0)[:n])
-
-        @pl.when(flipped)
-        def _():
-            cuts[w] = jnp.concatenate([planes[0].T, planes[1].T], axis=1)
-
-        @pl.when(jnp.logical_not(flipped))
-        def _():
-            cuts[w] = jnp.concatenate(planes, axis=1)
-
-        probe = probes[owners[0, 0, 0, w]]
-        starts[w] = jnp.concatenate([probe[0], probe[1]], axis=1)
+            block = pltpu.roll(padded[plane, rows, cols], lax.rem(2 * n - col_in, 2 * n), 1)[:, :n]
+            patches.append(pltpu.roll(block, lax.rem(n + 8 - row_in, n + 8), 0)[:n])
+    for k, probe in enumerate((first_probe, second_probe)):
+        starts[k] = jnp.concatenate([probe[0, 0], probe[0, 1]], axis=1)
+
+    @pl.when(flipped)
+    def _():
+        for k in range(2):
+            cuts[k] = jnp.concatenate([patches[2 * k].T, patches[2 * k + 1].T], axis=1)
+
+    @pl.when(jnp.logical_not(flipped))
+    def _():
+        for k in range(2):
+            cuts[k] = jnp.concatenate(patches[2 * k : 2 * k + 2], axis=1)
 
 
 def chain(
@@ -241,8 +240,9 @@
     phases, tables, cut, starts, measured,
     terms,
     forth_high, forth_low, back_high, back_low,
-    other, psis, turned_terms, waves_in, waves_out, turns_in, turns_out,
+    other, psis, turned_terms, waves_in, waves_out, turns_in, turns_out, targets,
     patch_sent, patch_got, wave_sent, wave_got, turn_sent, turn_got, term_sent, term_got,
+    start_got, target_got,
 ):
     n = tables.shape[0]
     place = lax.axis_index("depth")
@@ -282,13 +282,23 @@
     def _():
         pl.semaphore_signal(barrier, inc=1, device_id={"depth": place + 2}, device_id_type=MESH)
 
-    pl.semaphore_wait(barrier, 1 + jnp.where(before, 1, 0) + jnp.where(after, 1, 0))
-
-    @pl.when(jnp.logical_not(home))
+    def start_copy(j):
+        return pltpu.make_async_copy(starts.at[j], waves_in.at[j], start_got.at[j])
+
+    def target_copy(j):
+        return pltpu.make_async_copy(measured.at[j], targets.at[j], target_got.at[j])
+
+    @pl.when(home & (stage == 0))
     def _():
         @pl.loop(0, windows)
-        def _(w):
-            patch_copy(w).start()
+        def _(j):
+            start_copy(j).start()
+
+    @pl.when(home & (stage == last))
+    def _():
+        @pl.loop(0, windows)
+        def _(j):
+            target_copy(j).start()
 
     @pl.when(home)
     def _():
@@ -302,6 +312,14 @@
             keep_table(table[:, :n], table[:, n:], r, forth_high, forth_low)
             keep_table(table[:, :n], -table[:, n:], r, back_high, back_low)
 
+    pl.semaphore_wait(barrier, 1 + jnp.where(before, 1, 0) + jnp.where(after, 1, 0))
+
+    @pl.when(jnp.logical_not(home))
+    def _():
+        @pl.loop(0, windows)
+        def _(w):
+            patch_copy(w).start()
+
     def forth(wave, at):
         return both_sides(wave, forth_high[at], forth_low[at])
 
@@ -318,7 +336,7 @@
     def detect(j, wave):
         far = forth(wave, 2)
         real, imag = far[:, :n], far[:, n:]
-        excess = 2.0 * (real * real + imag * imag - measured[j].T)
+        excess = 2.0 * (real * real + imag * imag - targets[j].T)
         turns_in[j] = back(jnp.concatenate([excess * real, excess * imag], axis=1), 2)
 
     def second_term(j):
@@ -345,7 +363,7 @@
 
                 @pl.when(stage == 0)
                 def _():
-                    waves_in[t] = starts[t]
+                    start_copy(t).wait()
 
                 @pl.when(stage > 0)
                 def _():
@@ -386,6 +404,7 @@
     @pl.when(home & (stage == last))
     def _():
         def arrive(t):
+            target_copy(t).wait()
             patch_copy(t).wait_recv()
             wave_copy(t).wait_recv()
 
@@ -440,7 +459,7 @@
 
     @pl.loop(0, windows)
     def _(w):
-        row, col = centers[0, 0, 0, w], centers[0, 0, 1, w] + n // 2
+        row, col = centers[0, w], centers[1, w] + n // 2
         row_in, col_in = lax.rem(row, 8), lax.rem(col, 128)
         rows = pl.ds(pl.multiple_of(row - row_in, 8), n + 8)
         cols = pl.ds(pl.multiple_of(col - col_in, 128), 2 * n)
@@ -459,8 +478,8 @@
     half = n // 2
     measured = intensity[0, 0]
     windows = measured.shape[0]
-    places = jnp.transpose(centers, (0, 1, 3, 2))
-    owners = jnp.transpose(batch_of, (0, 1, 3, 2))
+    places = jnp.transpose(centers, (0, 1, 3, 2))[0, 0]
+    owners = jnp.transpose(batch_of, (0, 1, 3, 2))[0, 0]
     counts = jnp.arange(n, dtype=jnp.int32)
     angles = (counts[:, None] * counts[None, :] % n).astype(F32) * (2.0 * math.pi / n)
     tables = jnp.concatenate([jnp.cos(angles), jnp.sin(angles)], axis=1) * (1.0 / math.sqrt(n))
@@ -471,6 +490,7 @@
 
     smem = pl.BlockSpec(memory_space=pltpu.SMEM)
     vmem = pl.BlockSpec(memory_space=pltpu.VMEM)
+    stay = pl.BlockSpec(memory_space=pl.ANY)
     page = (n, 2 * n)
     dma = pltpu.SemaphoreType.DMA
     side = slices.shape[2]
@@ -495,24 +515,35 @@
         compiler_params=pltpu.CompilerParams(collective_id=1, has_side_effects=True),
     )(slices[0], phase)
 
+    probe_page = (1, 2, n, n)
+    pair = pl.BlockSpec((2, *page), lambda p, c, o: (p, 0, 0))
     cuts, starts = pl.pallas_call(
         gather,
         name="gather",
         out_shape=[jax.ShapeDtypeStruct((windows, *page), F32)] * 2,
-        in_specs=[smem, smem, vmem, vmem],
-        out_specs=[vmem, vmem],
-    )(places, owners, padded, probes)
+        grid_spec=pltpu.PrefetchScalarGridSpec(
+            num_scalar_prefetch=2,
+            grid=(windows // 2,),
+            in_specs=[
+                pl.BlockSpec(wide_shape.shape, lambda p, c, o: (0, 0, 0), pipeline_mode=pl.Buffered(1)),
+                pl.BlockSpec(probe_page, lambda p, c, o: (o[0, 2 * p], 0, 0, 0)),
+                pl.BlockSpec(probe_page, lambda p, c, o: (o[0, 2 * p + 1], 0, 0, 0)),
+            ],
+            out_specs=[pair, pair],
+        ),
+    )(places, owners, padded, probes, probes)
 
     terms = pl.pallas_call(
         functools.partial(chain, windows, sections // 2),
         name="chain",
         out_shape=jax.ShapeDtypeStruct((windows, *page), F32),
-        in_specs=[vmem] * 5,
+        in_specs=[vmem, vmem, vmem, stay, stay],
         out_specs=vmem,
         scratch_shapes=[pltpu.VMEM((3, 2 * n, 2 * n), BF16)] * 4
         + [pltpu.VMEM((windows, *page), F32), pltpu.VMEM((2, windows, *page), F32)]
         + [pltpu.VMEM((windows, *page), F32)] * 5
-        + [dma((windows,))] * 8,
+        + [pltpu.VMEM((windows, n, n), F32)]
+        + [dma((windows,))] * 10,
         compiler_params=pltpu.CompilerParams(collective_id=0, has_side_effects=True),
     )(phases, tables, cuts, starts, measured)
 

time: 179 us -> 179 us (level)
    pallas_call x1, Pallas kernels: 18.8 us -> 16.5 us  [local(): pl.pallas_call(fold, name='fold', out_shape=tile_shape, in_specs=[vmem],...]
where the time goes in v4:
time: 179 us
  Pallas kernels  174 us (97%)
  local copies, waits for them, and re-layouts  2.47 us (1%)
    pallas_call x1, Pallas kernels, local(): pl.pallas_call(functools.partial(chain, windows, sections // 2), name='ch...  129 us
    pallas_call x1, Pallas kernels, local(): pl.pallas_call(enlarge, name='enlarge', out_shape=[wide_shape, jax.ShapeD...  17.5 us
    pallas_call x1, Pallas kernels, local(): pl.pallas_call(fold, name='fold', out_shape=tile_shape, in_specs=[vmem],...  16.5 us
    pallas_call x1, Pallas kernels, local(): pl.pallas_call(gather, name='gather', out_shape=[jax.ShapeDtypeStruct((wi...  7.12 us
    pallas_call x1, Pallas kernels, local(): pl.pallas_call(spread, name='spread', out_shape=wide_shape, in_specs=[sme...  4.23 us

profile of v4, /device:TPU:1, one launch (start us, length us, event | category | flops | bytes accessed | tf_op | source)
XLA Modules:
  0.0 178.6 jit_solution(13537763204462055798)
XLA Ops:
  0.7 0.6 broadcast.59.phase
  1.3 17.5 %enlarge.1 = (f32[2,384,512]{2,1,0:T(8,128)}, f32[2,8,256]{2,1,0:T(8,128)}) custom-call(f32[2,256,256]{2,1,0:T(8,128)} %bitcast.10, f32[8,256]{1,0:T(8,128)} %broadcast.59.phase), custom_call_target="tpu_custom_call" | custom-call | tf_op jit(solution)/shard_map/enlarge/pallas_call | solution.py:508
  18.8 7.1 %gather.1 = (f32[12,128,256]{2,1,0:T(8,128)}, f32[12,128,256]{2,1,0:T(8,128)}) custom-call(s32[2,12]{1,0:T(2,128)} %bitcast.11, s32[1,12]{1,0:T(1,128)} %bitcast.13, f32[2,384,512]{2,1,0:T(8,128)} %get-tuple-element.10.padded, f32[8,2,128,128]{3,2,1,0:T(8,128)} %second_probe.1, f32[8,2,128,128]{3,2,1,0:T(8,128)} %second_probe.1), custom_call_target="tpu_custom_call" | custom-call | tf_op jit(solution)/shard_map/gather/pallas_call | solution.py:520
  25.9 0.3 fusion.6
  26.2 0.7 maximum_multiply_fusion.tables
  26.9 129.1 %chain.1.terms = f32[12,128,256]{2,1,0:T(8,128)} custom-call(f32[2,8,256]{2,1,0:T(8,128)} %get-tuple-element.9.phases, f32[128,256]{1,0:T(8,128)} %maximum_multiply_fusion.tables, f32[12,128,256]{2,1,0:T(8,128)} %get-tuple-element.11.cut, f32[12,128,256]{2,1,0:T(8,128)} %get-tuple-element.12.starts, f32[12,128,128]{2,1,0:T(8,128)} %bitcast.9), custom_call_target="tpu_custom_call" | custom-call | tf_op jit(solution)/shard_map/chain/pallas_call | solution.py:536
  156.0 4.2 %spread.1.total = f32[2,384,512]{2,1,0:T(8,128)} custom-call(s32[2,12]{1,0:T(2,128)} %bitcast.12, f32[12,128,256]{2,1,0:T(8,128)} %chain.1.terms), custom_call_target="tpu_custom_call" | custom-call | tf_op jit(solution)/shard_map/spread/pallas_call | solution.py:550
  160.2 16.5 %fold.1 = f32[2,256,256]{2,1,0:T(8,128)} custom-call(f32[2,384,512]{2,1,0:T(8,128)} %spread.1.total), custom_call_target="tpu_custom_call" | custom-call | tf_op jit(solution)/shard_map/fold/pallas_call | solution.py:558
  176.7 1.9 %copy.9 = f32[1,2,256,256]{3,2,1,0:T(8,128)} copy(f32[1,2,256,256]{3,2,1,0:T(8,128)} %bitcast.8) | data formatting | bytes 1048576
  (2 shorter events, 0.1 us)

commit v5 on v3

--- a/solution.py
+++ b/solution.py
@@ -212,28 +212,30 @@
     windows, n = cuts.shape[:2]
     flipped = lax.rem(lax.axis_index("depth"), 2) == 0
 
-    @pl.loop(0, windows)
-    def _(w):
-        row, col = centers[0, 0, 0, w], centers[0, 0, 1, w] + n // 2
-        row_in, col_in = lax.rem(row, 8), lax.rem(col, 128)
-        rows = pl.ds(pl.multiple_of(row - row_in, 8), n + 8)
-        cols = pl.ds(pl.multiple_of(col - col_in, 128), 2 * n)
-        planes = []
-        for plane in range(2):
-            block = padded[plane, rows, cols]
-            block = pltpu.roll(block, lax.rem(2 * n - col_in, 2 * n), 1)[:, :n]
-            planes.append(pltpu.roll(block, lax.rem(n + 8 - row_in, n + 8), 0)[:n])
+    @pl.loop(0, windows // 2)
+    def _(p):
+        patches = []
+        for k in range(2):
+            w = 2 * p + k
+            row, col = centers[0, 0, 0, w], centers[0, 0, 1, w] + n // 2
+            row_in, col_in = lax.rem(row, 8), lax.rem(col, 128)
+            rows = pl.ds(pl.multiple_of(row - row_in, 8), n + 8)
+            cols = pl.ds(pl.multiple_of(col - col_in, 128), 2 * n)
+            for plane in range(2):
+                block = pltpu.roll(padded[plane, rows, cols], lax.rem(2 * n - col_in, 2 * n), 1)[:, :n]
+                patches.append(pltpu.roll(block, lax.rem(n + 8 - row_in, n + 8), 0)[:n])
+            probe = probes[owners[0, 0, 0, w]]
+            starts[w] = jnp.concatenate([probe[0], probe[1]], axis=1)
 
         @pl.when(flipped)
         def _():
-            cuts[w] = jnp.concatenate([planes[0].T, planes[1].T], axis=1)
+            for k in range(2):
+                cuts[2 * p + k] = jnp.concatenate([patches[2 * k].T, patches[2 * k + 1].T], axis=1)
 
         @pl.when(jnp.logical_not(flipped))
         def _():
-            cuts[w] = jnp.concatenate(planes, axis=1)
-
-        probe = probes[owners[0, 0, 0, w]]
-        starts[w] = jnp.concatenate([probe[0], probe[1]], axis=1)
+            for k in range(2):
+                cuts[2 * p + k] = jnp.concatenate(patches[2 * k : 2 * k + 2], axis=1)
 
 
 def chain(
@@ -438,19 +440,21 @@
     windows, n = terms.shape[0], terms.shape[1]
     total[...] = jnp.zeros(total.shape, F32)
 
-    @pl.loop(0, windows)
-    def _(w):
-        row, col = centers[0, 0, 0, w], centers[0, 0, 1, w] + n // 2
-        row_in, col_in = lax.rem(row, 8), lax.rem(col, 128)
-        rows = pl.ds(pl.multiple_of(row - row_in, 8), n + 8)
-        cols = pl.ds(pl.multiple_of(col - col_in, 128), 2 * n)
-        term = terms[w]
+    @pl.loop(0, windows // 2)
+    def _(p):
         for plane in range(2):
-            block = term[:, plane * n : (plane + 1) * n]
-            block = jnp.concatenate([block, jnp.zeros((8, n), F32)], axis=0)
-            block = pltpu.roll(block, row_in, 0)
-            block = jnp.concatenate([block, jnp.zeros((n + 8, n), F32)], axis=1)
-            total[plane, rows, cols] += pltpu.roll(block, col_in, 1)
+            adds = []
+            for k in range(2):
+                w = 2 * p + k
+                row, col = centers[0, 0, 0, w], centers[0, 0, 1, w] + n // 2
+                row_in, col_in = lax.rem(row, 8), lax.rem(col, 128)
+                rows = pl.ds(pl.multiple_of(row - row_in, 8), n + 8)
+                cols = pl.ds(pl.multiple_of(col - col_in, 128), 2 * n)
+                block = jnp.concatenate([terms[w, :, plane * n : (plane + 1) * n], jnp.zeros((8, n), F32)], axis=0)
+                block = jnp.concatenate([pltpu.roll(block, row_in, 0), jnp.zeros((n + 8, n), F32)], axis=1)
+                adds.append((rows, cols, pltpu.roll(block, col_in, 1)))
+            for rows, cols, block in adds:
+                total[plane, rows, cols] += block
 
 
 def local(slices, thickness, probes, centers, batch_of, intensity):

time: 179 us -> 178 us (level)
    pallas_call x1, Pallas kernels: 127 us -> 131 us  [local(): pl.pallas_call(functools.partial(chain, windows, sections // 2), name='ch...]
    pallas_call x1, Pallas kernels: 18.8 us -> 16 us  [local(): pl.pallas_call(fold, name='fold', out_shape=tile_shape, in_specs=[vmem],...]
where the time goes in v5:
time: 178 us
  Pallas kernels  173 us (97%)
  local copies, waits for them, and re-layouts  2.47 us (1%)
    pallas_call x1, Pallas kernels, local(): pl.pallas_call(functools.partial(chain, windows, sections // 2), name='ch...  131 us
    pallas_call x1, Pallas kernels, local(): pl.pallas_call(enlarge, name='enlarge', out_shape=[wide_shape, jax.ShapeD...  17.5 us
    pallas_call x1, Pallas kernels, local(): pl.pallas_call(fold, name='fold', out_shape=tile_shape, in_specs=[vmem],...  16 us
    pallas_call x1, Pallas kernels, local(): pl.pallas_call(gather, name='gather', out_shape=[jax.ShapeDtypeStruct((wi...  5.49 us
    pallas_call x1, Pallas kernels, local(): pl.pallas_call(spread, name='spread', out_shape=wide_shape, in_specs=[sme...  3.78 us

profile of v5, /device:TPU:1, one launch (start us, length us, event | category | flops | bytes accessed | tf_op | source)
XLA Modules:
  0.0 177.6 jit_solution(1563840625040966250)
XLA Ops:
  0.7 0.6 broadcast.59.phase
  1.3 17.5 %enlarge.1 = (f32[2,384,512]{2,1,0:T(8,128)}, f32[2,8,256]{2,1,0:T(8,128)}) custom-call(f32[2,256,256]{2,1,0:T(8,128)} %bitcast.8, f32[8,256]{1,0:T(8,128)} %broadcast.59.phase), custom_call_target="tpu_custom_call" | custom-call | tf_op jit(solution)/shard_map/enlarge/pallas_call | solution.py:492
  18.8 5.5 %gather.1 = (f32[12,128,256]{2,1,0:T(8,128)}, f32[12,128,256]{2,1,0:T(8,128)}) custom-call(s32[1,1,2,12]{3,2,1,0:T(2,128)} %bitcast.9, s32[1,1,1,12]{3,2,1,0:T(1,128)} %bitcast.11, f32[2,384,512]{2,1,0:T(8,128)} %get-tuple-element.10.padded, f32[8,2,128,128]{3,2,1,0:T(8,128)} %probes.1), custom_call_target="tpu_custom_call" | custom-call | tf_op jit(solution)/shard_map/gather/pallas_call | solution.py:502
  24.3 0.3 fusion.6
  24.6 0.7 maximum_multiply_fusion.tables
  25.2 130.8 %chain.1.terms = f32[12,128,256]{2,1,0:T(8,128)} custom-call(f32[2,8,256]{2,1,0:T(8,128)} %get-tuple-element.9.phases, f32[128,256]{1,0:T(8,128)} %maximum_multiply_fusion.tables, f32[12,128,256]{2,1,0:T(8,128)} %get-tuple-element.11.cut, f32[12,128,256]{2,1,0:T(8,128)} %get-tuple-element.12.starts, f32[12,128,128]{2,1,0:T(8,128)} %bitcast.7), custom_call_target="tpu_custom_call" | custom-call | tf_op jit(solution)/shard_map/chain/pallas_call | solution.py:510
  156.0 3.8 %spread.1.total = f32[2,384,512]{2,1,0:T(8,128)} custom-call(s32[1,1,2,12]{3,2,1,0:T(2,128)} %bitcast.10, f32[12,128,256]{2,1,0:T(8,128)} %chain.1.terms), custom_call_target="tpu_custom_call" | custom-call | tf_op jit(solution)/shard_map/spread/pallas_call | solution.py:523
  159.8 16.0 %fold.1 = f32[2,256,256]{2,1,0:T(8,128)} custom-call(f32[2,384,512]{2,1,0:T(8,128)} %spread.1.total), custom_call_target="tpu_custom_call" | custom-call | tf_op jit(solution)/shard_map/fold/pallas_call | solution.py:531
  175.8 1.9 %copy.9 = f32[1,2,256,256]{3,2,1,0:T(8,128)} copy(f32[1,2,256,256]{3,2,1,0:T(8,128)} %bitcast.6) | data formatting | bytes 1048576
  (2 shorter events, 0.1 us)
